TPU v7x, 8 devices: a whole 2x2x1 slice. The times are simulated.
8 devices in a mesh: rep: 2 (over y, z), dp: 4 (over x, core).
Axes of the slice: x: 2, y: 2, z: 1, core: 2. Of those that a mesh axis runs over, the one named last changes fastest.
Arguments:
- x: bfloat16 [8, 2048, 1024], P(('rep', 'dp')), parts along dimension 0
- dy: bfloat16 [8, 2048, 1024], P(('rep', 'dp')), parts along dimension 0
- w_gate: bfloat16 [2, 1024, 2816], replicated
- w_up: bfloat16 [2, 1024, 2816], replicated
- w_down: bfloat16 [2, 2816, 1024], replicated
- m_w_gate: float32 [2, 1024, 2816], replicated
- m_w_up: float32 [2, 1024, 2816], replicated
- m_w_down: float32 [2, 2816, 1024], replicated
- v_w_gate: float32 [2, 1024, 2816], replicated
- v_w_up: float32 [2, 1024, 2816], replicated
- v_w_down: float32 [2, 2816, 1024], replicated
Outputs:
- output 1: bfloat16 [4, 1024, 2816], P('rep'), parts along dimension 0
- output 2: bfloat16 [4, 1024, 2816], P('rep'), parts along dimension 0
- output 3: bfloat16 [4, 2816, 1024], P('rep'), parts along dimension 0
- output 4: float32 [4, 1024, 2816], P('rep'), parts along dimension 0
- output 5: float32 [4, 1024, 2816], P('rep'), parts along dimension 0
- output 6: float32 [4, 2816, 1024], P('rep'), parts along dimension 0
- output 7: float32 [4, 1024, 2816], P('rep'), parts along dimension 0
- output 8: float32 [4, 1024, 2816], P('rep'), parts along dimension 0
- output 9: float32 [4, 2816, 1024], P('rep'), parts along dimension 0
There are 2 independent parts. A program takes and returns all parts, laid end to end along the dimension named above; an argument that names none is the same for every part.
All inputs are finite; a program needn't handle non-finite values.
Results may differ from a plain program's by a relative error of at most 0.022.
Values are sent between devices in bfloat16 or wider.
A program may use at most 2.75 GiB of HBM per device.

v0:
```python
import jax
import jax.numpy as jnp
from jax import lax
from jax.sharding import PartitionSpec as P

NAMES = ("w_gate", "w_up", "w_down")


def matmul(a, w):
    return jnp.dot(a, w, preferred_element_type=jnp.float32).astype(jnp.bfloat16)


def normed(h):
    wide = h.astype(jnp.float32)
    scale = lax.rsqrt(jnp.mean(wide**2, -1, keepdims=True) + 1e-6)
    return (wide * scale).astype(jnp.bfloat16)


def layer(h, w):
    a = normed(h)
    gate = jnp.dot(a, w["w_gate"], preferred_element_type=jnp.float32)
    up = jnp.dot(a, w["w_up"], preferred_element_type=jnp.float32)
    return h + matmul((jax.nn.silu(gate) * up).astype(jnp.bfloat16), w["w_down"])


def adamw(w, m, v, g):
    m = 0.9 * m + 0.1 * g
    v = 0.95 * v + 0.05 * g * g
    step = m * lax.rsqrt(v + 1e-8) + 0.1 * w
    return (w - 0.02 * step).astype(jnp.bfloat16), m, v


def clipped(gradients, sum_of_squares, count):
    factor = jnp.minimum(1.0, 0.5 * lax.rsqrt(sum_of_squares / count + 1e-30))
    return [g * factor for g in gradients]


def solution(mesh):
    def step(x, dy, *arrays):
        weights, m, v = (arrays[i : i + 3] for i in (0, 3, 6))
        layers = weights[0].shape[0]
        h, kept = x[0], []
        for number in range(layers):
            kept.append(h)
            h = layer(h, {name: w[number] for name, w in zip(NAMES, weights, strict=True)})
        by_h, summed = dy[0], [None] * layers
        for number in reversed(range(layers)):
            _, back = jax.vjp(lambda w, h: layer(h, w), {name: w[number] for name, w in zip(NAMES, weights, strict=True)}, kept[number])
            by_w, by_h = back(by_h)
            summed[number] = [lax.psum(by_w[name], "dp") for name in NAMES]
        gradients = [jnp.stack([summed[number][i] for number in range(layers)]).astype(jnp.float32) for i in range(3)]
        gradients = clipped(gradients, sum(jnp.sum(g * g) for g in gradients), sum(g.size for g in gradients))
        new = [adamw(w.astype(jnp.float32), m, v, g) for w, m, v, g in zip(weights, m, v, gradients, strict=True)]
        return tuple(one[which] for which in range(3) for one in new)

    return jax.shard_map(
        step,
        mesh=mesh,
        in_specs=(P(("rep", "dp"), None, None),) * 2 + (P(None, None, None),) * 9,
        out_specs=(P("rep", None, None),) * 9,
        check_vma=False,
    )
```

profile of v0, /device:TPU:0, one launch (start us, length us, event | category | flops | bytes accessed | tf_op | source)
XLA Modules:
  0.0 1092.6 jit_solution(8517558870146898274)
XLA Ops:
  7.2 0.0 all-reduce.3.cloned.1.call-start
  7.2 6.5 copy.20
  13.7 3.1 fusion.36
  16.8 0.0 copy-start.7
  16.8 6.5 copy.21
  23.3 0.0 copy-start.4
  23.3 18.3 %convolution_convert_fusion.1 = bf16[2048,2816]{1,0:T(8,128)(2,1)} fusion(bf16[2,2816,1024]{2,1,0:T(8,128)(2,1)} %param.15, bf16[1,2048,1024]{2,1,0:T(8,128)(2,1)} %param.12), kind=kOutput, calls=%fused_computation.68 | convolution fusion | flops 11816927232 | bytes 21495808 | tf_op jit(solution)/shard_map/transpose(jvp())/dot_general | solution.py:10
  41.6 0.0 copy-done.4
  41.6 18.3 %fusion.56 = f32[2048,2816]{1,0:T(8,128)} fusion(bf16[2,1024,2816]{2,1,0:T(8,128)(2,1)} %param.13, bf16[1,2048,1024]{2,1,0:T(8,128)(2,1)S(1)} %copy-done.4, f32[2048]{0:T(1024)S(1)} %add_rsqrt_fusion), kind=kOutput, calls=%fused_computation.93 | convolution fusion | flops 11817451520 | bytes 33038336 | tf_op jit(solution)/shard_map/dot_general | solution.py:21
  59.9 0.0 copy-done.7
  59.9 28.7 %multiply_convert_fusion.1 = (bf16[2048,2816]{1,0:T(8,128)(2,1)}, f32[2048,2816]{1,0:T(8,128)}) fusion(f32[2048,2816]{1,0:T(8,128)} %fusion.56, bf16[2,1024,2816]{2,1,0:T(8,128)(2,1)} %param.14, bf16[1,2048,1024]{2,1,0:T(8,128)(2,1)} %param.11, f32[2048]{0:T(1024)S(1)} %add_rsqrt_fusion), kind=kOutput, calls=%fused_computation.53 | convolution fusion | flops 11852054528 | bytes 67641344 | tf_op jit(solution)/shard_map/dot_general | solution.py:22
  88.6 19.7 %fusion.40 = (f32[2048]{0:T(1024)S(1)}, bf16[2048,1024]{0,1:T(8,128)(2,1)}) fusion(bf16[2048,2816]{1,0:T(8,128)(2,1)} %get-tuple-element.24, bf16[2,2816,1024]{2,1,0:T(8,128)(2,1)} %param.15, bf16[1,2048,1024]{1,2,0:T(8,128)(2,1)} %copy.20), kind=kOutput, calls=%fused_computation.76 | convolution fusion | flops 11821643776 | bytes 25698304 | tf_op jit(solution)/shard_map/dot_general | solution.py:10
  108.3 0.0 copy-start.5
  108.3 0.6 copy-done.5
  108.9 0.0 copy-start.1
  108.9 20.3 %fusion.43 = f32[2048,2816]{1,0:T(8,128)} fusion(bf16[2,1024,2816]{2,1,0:T(8,128)(2,1)} %param.14, bf16[2048,1024]{0,1:T(8,128)(2,1)} %get-tuple-element.27, f32[2048]{0:T(1024)S(1)} %fusion.86), kind=kOutput, calls=%fused_computation.80 | convolution fusion | flops 11817451520 | bytes 33038336 | tf_op jit(solution)/shard_map/jvp()/dot_general | solution.py:22
  129.2 0.0 copy-done.1
  129.2 31.5 %fusion.20 = (bf16[2048,2816]{1,0:T(8,128)(2,1)}, f32[2048,2816]{1,0:T(8,128)}) fusion(f32[2048,2816]{1,0:T(8,128)} %fusion.43, bf16[2048,2816]{1,0:T(8,128)(2,1)} %convolution_convert_fusion.1, bf16[2,1024,2816]{2,1,0:T(8,128)(2,1)} %param.13, bf16[2048,1024]{0,1:T(8,128)(2,1)S(1)} %copy-done.1, f32[2048]{0:T(1024)S(1)} %fusion.86), kind=kOutput, calls=%fused_computation.41 | convolution fusion | flops 11886657536 | bytes 79175680 | tf_op jit(solution)/shard_map/jvp()/dot_general | solution.py:21
  160.8 20.2 %fusion.33 = bf16[2048,1024]{0,1:T(8,128)(2,1)} fusion(bf16[2048,2816]{1,0:T(8,128)(2,1)} %convolution_convert_fusion.1, bf16[2,1024,2816]{2,1,0:T(8,128)(2,1)} %param.14, f32[2048,2816]{1,0:T(8,128)} %get-tuple-element.29), kind=kOutput, calls=%fused_computation.57 | convolution fusion | flops 11845763072 | bytes 44564480 | tf_op jit(solution)/shard_map/transpose(jvp())/dot_general | solution.py:22
  181.0 22.3 %convert_bitcast_fusion.2 = bf16[1,1024,2816]{2,1,0:T(8,128)(2,1)} fusion(bf16[2048,2816]{1,0:T(8,128)(2,1)} %convolution_convert_fusion.1, bf16[2048,1024]{0,1:T(8,128)(2,1)} %get-tuple-element.27, f32[2048]{0:T(1024)S(1)} %fusion.86, f32[2048,2816]{1,0:T(8,128)} %get-tuple-element.29), kind=kOutput, calls=%fused_computation.97 | convolution fusion | flops 11854938112 | bytes 44572672 | tf_op jit(solution)/shard_map/transpose(jvp())/dot_general | solution.py:22
  203.3 0.0 copy-start.2
  203.3 23.8 %convert_bitcast_fusion = bf16[1,2816,1024]{2,1,0:T(8,128)(2,1)} fusion(f32[2048,2816]{1,0:T(8,128)} %fusion.43, bf16[1,2048,1024]{2,1,0:T(8,128)(2,1)} %param.12, f32[2048,2816]{1,0:T(8,128)} %get-tuple-element.29), kind=kOutput, calls=%fused_computation.95 | convolution fusion | flops 11848646656 | bytes 56098816 | tf_op jit(solution)/shard_map/transpose(jvp())/dot_general | solution.py:10
  227.2 0.0 copy-done.2
  227.2 17.5 %convert_bitcast_fusion.4 = bf16[1,1024,2816]{2,1,0:T(8,128)(2,1)} fusion(bf16[2048,2816]{1,0:T(8,128)(2,1)} %get-tuple-element.28, bf16[2048,1024]{0,1:T(8,128)(2,1)S(1)} %copy-done.2, f32[2048]{0:T(1024)S(1)} %fusion.86), kind=kOutput, calls=%fused_computation.99 | convolution fusion | flops 11817451520 | bytes 21504000 | tf_op jit(solution)/shard_map/transpose(jvp())/dot_general | solution.py:21
  244.7 0.0 copy-start.6
  244.7 0.0 copy-start
  244.7 19.6 %fusion.42 = (f32[2048]{0:T(1024)S(1)}, bf16[2048,1024]{0,1:T(8,128)(2,1)}) fusion(bf16[2048,1024]{0,1:T(8,128)(2,1)S(1)} %copy-done.2, bf16[2048,1024]{0,1:T(8,128)(2,1)} %fusion.33, bf16[2048,2816]{1,0:T(8,128)(2,1)} %get-tuple-element.28, bf16[2,1024,2816]{2,1,0:T(8,128)(2,1)} %param.13), kind=kOutput, calls=%fused_computation.78 | convolution fusion | flops 11821643776 | bytes 29892608 | tf_op jit(solution)/shard_map/transpose(jvp())/dot_general | solution.py:21
  264.3 0.0 copy-done.6
  264.4 0.0 copy-done
  264.4 6.0 fusion.70
  270.4 0.0 copy-start.3
  270.4 18.4 %convolution_convert_fusion = bf16[2048,2816]{1,0:T(8,128)(2,1)} fusion(bf16[2048,1024]{0,1:T(8,128)(2,1)} %fusion.70, bf16[2,2816,1024]{2,1,0:T(8,128)(2,1)} %param.15), kind=kOutput, calls=%fused_computation.67 | convolution fusion | flops 11816927232 | bytes 21495808 | tf_op jit(solution)/shard_map/transpose(jvp())/dot_general | solution.py:10
  288.8 0.0 copy-done.3
  288.8 0.0 copy-start.8
  288.8 17.0 %convert_bitcast_fusion.1 = bf16[1,2816,1024]{2,1,0:T(8,128)(2,1)} fusion(bf16[2048,2816]{1,0:T(8,128)(2,1)} %get-tuple-element.24, bf16[2048,1024]{0,1:T(8,128)(2,1)S(1)} %copy-done.3), kind=kOutput, calls=%fused_computation.96 | convolution fusion | flops 11814043648 | bytes 21495808 | tf_op jit(solution)/shard_map/transpose(jvp())/dot_general | solution.py:10
  305.8 0.0 copy-done.8
  305.8 22.3 %convert_bitcast_fusion.3 = bf16[1,1024,2816]{2,1,0:T(8,128)(2,1)} fusion(bf16[2048,2816]{1,0:T(8,128)(2,1)} %convolution_convert_fusion, f32[2048,2816]{1,0:T(8,128)} %fusion.56, bf16[1,2048,1024]{1,2,0:T(8,128)(2,1)} %copy.20, f32[2048]{0:T(1024)S(1)} %copy-done.8), kind=kOutput, calls=%fused_computation.98 | convolution fusion | flops 11854938112 | bytes 44572672 | tf_op jit(solution)/shard_map/transpose(jvp())/dot_general | solution.py:22
  328.1 27.0 %convert_bitcast_fusion.5 = bf16[1,1024,2816]{2,1,0:T(8,128)(2,1)} fusion(f32[2048,2816]{1,0:T(8,128)} %fusion.56, f32[2048,2816]{1,0:T(8,128)} %get-tuple-element.25, bf16[2048,2816]{1,0:T(8,128)(2,1)} %convolution_convert_fusion, bf16[1,2048,1024]{1,2,0:T(8,128)(2,1)} %copy.20, f32[2048]{0:T(1024)S(1)} %copy-done.8), kind=kOutput, calls=%fused_computation.100 | convolution fusion | flops 11883773952 | bytes 67641344 | tf_op jit(solution)/shard_map/transpose(jvp())/dot_general | solution.py:21
  355.1 0.0 all-reduce.3.cloned.1.call-update
  355.1 573.3 %all-reduce.3.cloned.1.call-done = (bf16[1,1024,2816]{2,1,0:T(8,128)(2,1)}, bf16[1,1024,2816]{2,1,0:T(8,128)(2,1)}, bf16[1,1024,2816]{2,1,0:T(8,128)(2,1)}, bf16...) async-done(((bf16[1,1024,2816]{2,1,0:T(8,128)(2,1)}, bf16[1,1024,2816]{2,1,0:T(8,128)(2,1)}, ...) | async-done | bytes 34603024 | tf_op jit(solution)/shard_map/psum | solution.py:50
  928.5 0.0 slice-start.2
  928.5 0.0 slice-start.3
  928.5 11.0 %fusion.10 = f32[]{:T(128)} fusion(bf16[1,1024,2816]{2,1,0:T(8,128)(2,1)} %get-tuple-element.9, bf16[1,1024,2816]{2,1,0:T(8,128)(2,1)} %get-tuple-element.10), kind=kLoop, calls=%fused_computation.31 | loop fusion | flops 23068672 | bytes 11534340 | tf_op jit(solution)/shard_map/reduce_sum | solution.py:52
  939.5 0.0 slice-done.2
  939.5 0.0 slice-done.3
  939.5 9.2 fusion.11
  949.9 0.0 slice-start
  949.9 11.2 %fusion.12 = f32[]{:T(128)} fusion(bf16[1,2816,1024]{2,1,0:T(8,128)(2,1)} %get-tuple-element.13, bf16[1,2816,1024]{2,1,0:T(8,128)(2,1)} %get-tuple-element.14), kind=kLoop, calls=%fused_computation.33 | loop fusion | flops 23068672 | bytes 11534340 | tf_op jit(solution)/shard_map/reduce_sum | solution.py:52
  961.9 0.0 slice-start.1
  961.9 40.7 %fusion.18 = (bf16[2,2816,1024]{2,1,0:T(8,128)(2,1)}, f32[2,2816,1024]{2,1,0:T(8,128)}, f32[2,2816,1024]{2,1,0:T(8,128)}) fusion(bf16[2,2816,1024]{2,1,0:T(8,128)(2,1)} %param.15, f32[]{:T(128)S(6)} %min_shard_map.3, bf16[1,2816,1024]{2,1,0:T(8,128)(2,1)} %get-tuple-element.13, bf16[1,2816,1024]{2,1,0:T(8,128)(2,1)} %get-tuple-element.14, ...), kind=kLoop, calls=%fused_computation.39 | loop fusion | flops 115343360 | bytes 126877696 | tf_op jit(solution)/shard_map/convert_element_type | solution.py:30
  1002.6 0.0 slice-done
  1002.6 0.0 slice-done.1
  1002.6 82.7 %fusion.8 = (bf16[2,1024,2816]{2,1,0:T(8,128)(2,1)}, f32[2,1024,2816]{2,1,0:T(8,128)}, f32[2,1024,2816]{2,1,0:T(8,128)}, bf16[2,1024,2816]{2,1,0:T(8,128)(2,1)},...) fusion(bf16[2,1024,2816]{2,1,0:T(8,128)(2,1)} %param.13, f32[]{:T(128)S(6)} %min_shard_map.3, ...), kind=kLoop, calls=%fused_computation.29 | loop fusion | flops 230686720 | bytes 253755392 | tf_op jit(solution)/shard_map/convert_element_type | solution.py:30
  (5 shorter events, 0.0 us)
Async XLA Ops:
  7.2 921.3 %all-reduce.3.cloned.1.call-start = ((), (), s32[]{:S(2)}) async-start(), calls=%async_computation | async-start | bytes 69206016 | tf_op jit(solution)/shard_map/psum | solution.py:50
  16.8 43.1 %copy-start.7 = (f32[2048]{0:T(1024)}, f32[2048]{0:T(1024)S(1)}, u32[]{:S(2)}) copy-start(f32[2048]{0:T(1024)S(1)} %add_rsqrt_fusion) | copy-start | bytes 24580
  23.3 18.3 %copy-start.4 = (bf16[1,2048,1024]{2,1,0:T(8,128)(2,1)S(1)}, bf16[1,2048,1024]{2,1,0:T(8,128)(2,1)}, u32[]{:S(2)}) copy-start(bf16[1,2048,1024]{2,1,0:T(8,128)(2,1)} %param.11) | copy-start | bytes 12582916
  108.3 0.6 copy-start.5
  108.9 20.3 %copy-start.1 = (bf16[2048,1024]{0,1:T(8,128)(2,1)S(1)}, bf16[2048,1024]{0,1:T(8,128)(2,1)}, u32[]{:S(2)}) copy-start(bf16[2048,1024]{0,1:T(8,128)(2,1)} %get-tuple-element.27) | copy-start | bytes 12582916
  203.3 23.9 %copy-start.2 = (bf16[2048,1024]{0,1:T(8,128)(2,1)S(1)}, bf16[2048,1024]{0,1:T(8,128)(2,1)}, u32[]{:S(2)}) copy-start(bf16[2048,1024]{0,1:T(8,128)(2,1)} %get-tuple-element.27) | copy-start | bytes 12582916
  244.7 19.6 %copy-start.6 = (f32[2048]{0:T(1024)S(1)}, f32[2048]{0:T(1024)}, u32[]{:S(2)}) copy-start(f32[2048]{0:T(1024)} %copy-done.5) | copy-start | bytes 24580
  244.7 19.7 %copy-start = (bf16[1,2048,1024]{1,2,0:T(8,128)(2,1)S(1)}, bf16[1,2048,1024]{1,2,0:T(8,128)(2,1)}, u32[]{:S(2)}) copy-start(bf16[1,2048,1024]{1,2,0:T(8,128)(2,1)} %copy.21) | copy-start | bytes 12582916
  270.4 18.4 %copy-start.3 = (bf16[2048,1024]{0,1:T(8,128)(2,1)S(1)}, bf16[2048,1024]{0,1:T(8,128)(2,1)}, u32[]{:S(2)}) copy-start(bf16[2048,1024]{0,1:T(8,128)(2,1)} %fusion.70) | copy-start | bytes 12582916
  288.8 17.0 %copy-start.8 = (f32[2048]{0:T(1024)S(1)}, f32[2048]{0:T(1024)}, u32[]{:S(2)}) copy-start(f32[2048]{0:T(1024)} %copy-done.7) | copy-start | bytes 24580
  928.5 11.0 %slice-start.2 = ((s8[5767168]{0:T(1024)(128)(4,1)}), s8[4194304]{0:T(1024)(128)(4,1)S(1)}, s32[]{:S(2)}) async-start(s8[5767168]{0:T(1024)(128)(4,1)} %bitcast.76), calls=%async_computation.3 | async-start | bytes 8388608
  928.5 11.0 %slice-start.3 = ((s8[5767168]{0:T(1024)(128)(4,1)}), s8[1572864]{0:T(1024)(128)(4,1)S(1)}, s32[]{:S(2)}) async-start(s8[5767168]{0:T(1024)(128)(4,1)} %bitcast.76), calls=%async_computation.4 | async-start | bytes 3145728
  949.9 52.7 %slice-start = ((s8[5767168]{0:T(1024)(128)(4,1)}), s8[1572864]{0:T(1024)(128)(4,1)S(1)}, s32[]{:S(2)}) async-start(s8[5767168]{0:T(1024)(128)(4,1)} %bitcast.74), calls=%async_computation.1 | async-start | bytes 3145728
  961.9 40.7 %slice-start.1 = ((s8[5767168]{0:T(1024)(128)(4,1)}), s8[4194304]{0:T(1024)(128)(4,1)S(1)}, s32[]{:S(2)}) async-start(s8[5767168]{0:T(1024)(128)(4,1)} %bitcast.74), calls=%async_computation.2 | async-start | bytes 8388608
Sparse Core Ops, SparseCore 0:
  355.2 573.1 all-reduce.2
where the time goes:
time: 1100 us; the launch traced here: 1090 us
  waiting for transfers between devices  573 us (52%)
  matrix products  325 us (30%)
  other arithmetic  164 us (15%)
  between operations  16.6 us (2%)
  local copies, waits for them, and re-layouts  13.7 us (1%)
    psum x1, waiting for transfers between devices, step(): summed[number] = [lax.psum(by_w[name], 'dp') for name in NAMES]  573 us
    convert_element_type x2, other arithmetic, adamw(): return ((w - 0.02 * step).astype(jnp.bfloat16), m, v)  123 us
    dot_general x5, matrix products, layer(): gate = jnp.dot(a, w['w_gate'], preferred_element_type=jnp.float32)  114 us
    dot_general x5, matrix products, layer(): up = jnp.dot(a, w['w_up'], preferred_element_type=jnp.float32)  114 us
    dot_general x5, matrix products, matmul(): jnp.dot(a, w, preferred_element_type=jnp.float32).astype(jnp.bfloat16)  97.2 us
    reduce_sum x3, other arithmetic, step(): jnp.sum(g * g)  31.4 us
  transfers between devices with their start and end apart: 1, of which 1 were waited for; matrix products, arithmetic and copies ran while one was open for 0% of the time, Pallas kernels for 0%

commit v1 on v0

v1 whole, which is shorter than its diff:
```python
import functools

import jax
import jax.numpy as jnp
import numpy as np
from jax import lax
from jax.experimental import pallas as pl
from jax.experimental.pallas import tpu as pltpu
from jax.sharding import PartitionSpec as P

BF, F32 = jnp.bfloat16, jnp.float32
T, D, FF = 2048, 1024, 2816
FT = 256
NT = FF // FT
HALF, QUARTER = D // 2, D // 4
CHUNK = 512
NC = T // CHUNK
X_SWAP = [(0, 2), (2, 0), (1, 3), (3, 1)]
CORE_SWAP = [(0, 1), (1, 0), (2, 3), (3, 2)]
VMEM_LIMIT = 64 * 1000 * 1000
EPS = 1e-6


def dot(a, b):
    return jnp.dot(a, b, preferred_element_type=F32)


def dot_nt(a, b):
    return lax.dot_general(a, b, (((1,), (1,)), ((), ())), preferred_element_type=F32)


def params(n=1):
    return pltpu.CompilerParams(dimension_semantics=("arbitrary",) * n, vmem_limit_bytes=VMEM_LIMIT)


def cost(matmuls, nbytes):
    return pl.CostEstimate(flops=int(matmuls * 2 * T * D * FF), bytes_accessed=int(nbytes), transcendentals=0)


def norm(h):
    wide = h.astype(F32)
    return wide * lax.rsqrt(jnp.mean(wide * wide, -1, keepdims=True) + EPS)


def whole(shape):
    return pl.BlockSpec(shape, lambda *_: (0,) * len(shape))


def gate_up_kernel(h_ref, wg_ref, wu_ref, act_ref, gate_ref, up_ref, at_ref, a_ref):
    @pl.when(pl.program_id(0) == 0)
    def _():
        for r in range(NC):
            rows = slice(r * CHUNK, (r + 1) * CHUNK)
            a = norm(h_ref[rows, :]).astype(BF)
            a_ref[rows, :] = a
            at_ref[:, rows] = a.T

    for r in range(NC):
        rows = slice(r * CHUNK, (r + 1) * CHUNK)
        gate = dot(a_ref[rows, :], wg_ref[...])
        up = dot(a_ref[rows, :], wu_ref[...])
        gate_ref[rows, :] = gate
        up_ref[rows, :] = up
        act_ref[rows, :] = (gate * jax.nn.sigmoid(gate) * up).astype(BF)


def gate_up(h, wg, wu, layer):
    weight = pl.BlockSpec((None, D, FT), lambda j: (layer, 0, j))
    tile = pl.BlockSpec((T, FT), lambda j: (0, j))
    return pl.pallas_call(
        gate_up_kernel,
        grid=(NT,),
        in_specs=[whole((T, D)), weight, weight],
        out_specs=[tile, tile, tile, whole((D, T))],
        out_shape=[
            jax.ShapeDtypeStruct((T, FF), BF),
            jax.ShapeDtypeStruct((T, FF), F32),
            jax.ShapeDtypeStruct((T, FF), F32),
            jax.ShapeDtypeStruct((D, T), BF),
        ],
        scratch_shapes=[pltpu.VMEM((T, D), BF)],
        compiler_params=params(),
        cost_estimate=cost(2, 75e6),
        name="gate_up",
    )(h, wg, wu)


def down_kernel(act_ref, w_ref, h_ref, out_ref, a_ref, at_ref):
    h = h_ref[...] + dot(act_ref[...], w_ref[...]).astype(BF)
    out_ref[...] = h
    a = norm(h).astype(BF)
    a_ref[...] = a
    at_ref[...] = a.T


def down(act, w, h, layer):
    rows = pl.BlockSpec((CHUNK, D), lambda i: (i, 0))
    return pl.pallas_call(
        down_kernel,
        grid=(NC,),
        in_specs=[
            pl.BlockSpec((CHUNK, FF), lambda i: (i, 0)),
            pl.BlockSpec((None, FF, D), lambda i: (layer, 0, 0)),
            rows,
        ],
        out_specs=[rows, rows, pl.BlockSpec((D, CHUNK), lambda i: (0, i))],
        out_shape=[
            jax.ShapeDtypeStruct((T, D), BF),
            jax.ShapeDtypeStruct((T, D), BF),
            jax.ShapeDtypeStruct((D, T), BF),
        ],
        compiler_params=params(),
        cost_estimate=cost(1, 30e6),
        name="down",
    )(act, w, h)


def turn_kernel(x_ref, xt_ref):
    xt_ref[...] = x_ref[...].T


def norm_turn_kernel(h_ref, x_ref, a_ref, at_ref, xt_ref):
    a = norm(h_ref[...]).astype(BF)
    a_ref[...] = a
    at_ref[...] = a.T
    xt_ref[...] = x_ref[...].T


def turn(x):
    return pl.pallas_call(
        turn_kernel,
        grid=(NC,),
        in_specs=[pl.BlockSpec((CHUNK, D), lambda i: (i, 0))],
        out_specs=pl.BlockSpec((D, CHUNK), lambda i: (0, i)),
        out_shape=jax.ShapeDtypeStruct((D, T), BF),
        compiler_params=params(),
        cost_estimate=cost(0.2, 8e6),
        name="turn",
    )(x)


def norm_turn(h, x):
    rows = pl.BlockSpec((CHUNK, D), lambda i: (i, 0))
    columns = pl.BlockSpec((D, CHUNK), lambda i: (0, i))
    return pl.pallas_call(
        norm_turn_kernel,
        grid=(NC,),
        in_specs=[rows, rows],
        out_specs=[rows, columns, columns],
        out_shape=[jax.ShapeDtypeStruct((T, D), BF), jax.ShapeDtypeStruct((D, T), BF), jax.ShapeDtypeStruct((D, T), BF)],
        compiler_params=params(),
        cost_estimate=cost(0.4, 20e6),
        name="norm_turn",
    )(h, x)


def gated(gate, up, by_act):
    by_act = by_act.astype(BF).astype(F32)
    sig = jax.nn.sigmoid(gate)
    silu = gate * sig
    by_gate = by_act * up * (sig + silu * (1.0 - sig))
    return (silu * up).astype(BF), by_gate.astype(BF), (by_act * silu).astype(BF)


def hidden_kernel(a_ref, by_ref, wg_ref, wu_ref, wd_ref, act_ref, dg_ref, du_ref):
    for r in range(NC):
        rows = slice(r * CHUNK, (r + 1) * CHUNK)
        gate = dot(a_ref[rows, :], wg_ref[...])
        up = dot(a_ref[rows, :], wu_ref[...])
        by_act = dot_nt(by_ref[rows, :], wd_ref[...])
        act_ref[rows, :], dg_ref[rows, :], du_ref[rows, :] = gated(gate, up, by_act)


def hidden(a, by, wg, wu, wd, layer):
    weight = pl.BlockSpec((None, D, FT), lambda j: (layer, 0, j))
    tile = pl.BlockSpec((T, FT), lambda j: (0, j))
    return pl.pallas_call(
        hidden_kernel,
        grid=(NT,),
        in_specs=[whole((T, D)), whole((T, D)), weight, weight, pl.BlockSpec((None, FT, D), lambda j: (layer, j, 0))],
        out_specs=[tile, tile, tile],
        out_shape=[jax.ShapeDtypeStruct((T, FF), BF)] * 3,
        compiler_params=params(),
        cost_estimate=cost(3, 60e6),
        name="hidden",
    )(a, by, wg, wu, wd)


def states_kernel(dg_ref, du_ref, wg_ref, wu_ref, h_ref, by_ref, out_ref, outt_ref):
    by_a = dot_nt(dg_ref[...], wg_ref[...]).astype(BF) + dot_nt(du_ref[...], wu_ref[...]).astype(BF)
    wide = h_ref[...].astype(F32)
    by_a = by_a.astype(F32)
    scale = lax.rsqrt(jnp.mean(wide * wide, -1, keepdims=True) + EPS)
    inner = jnp.mean(by_a * wide, -1, keepdims=True)
    by_h = by_a * scale - wide * (inner * scale * scale * scale)
    out = by_ref[...] + by_h.astype(BF)
    out_ref[...] = out
    outt_ref[...] = out.T


def states(dg, du, wg, wu, h, by, layer):
    tm = 256
    rows = pl.BlockSpec((tm, D), lambda i: (i, 0))
    hidden_rows = pl.BlockSpec((tm, FF), lambda i: (i, 0))
    weight = pl.BlockSpec((None, D, FF), lambda i: (layer, 0, 0))
    return pl.pallas_call(
        states_kernel,
        grid=(T // tm,),
        in_specs=[hidden_rows, hidden_rows, weight, weight, rows, rows],
        out_specs=[rows, pl.BlockSpec((D, tm), lambda i: (0, i))],
        out_shape=[jax.ShapeDtypeStruct((T, D), BF), jax.ShapeDtypeStruct((D, T), BF)],
        compiler_params=params(),
        cost_estimate=cost(2, 45e6),
        name="states",
    )(dg, du, wg, wu, h, by)


def halves(core_ref):
    keep = pl.ds(pl.multiple_of(core_ref[0] * HALF, HALF), HALF)
    send = pl.ds(pl.multiple_of((1 - core_ref[0]) * HALF, HALF), HALF)
    return keep, send


def first_weights_kernel(core_ref, at_ref, byt_ref, by_ref, gate_ref, up_ref, wd_ref, keep_ref, send_ref, act_ref, dg_ref, du_ref):
    for r in range(NC):
        rows = slice(r * CHUNK, (r + 1) * CHUNK)
        by_act = dot_nt(by_ref[rows, :], wd_ref[...])
        act_ref[rows, :], dg_ref[rows, :], du_ref[rows, :] = gated(gate_ref[rows, :], up_ref[rows, :], by_act)
    keep, send = halves(core_ref)
    for half, out_ref in ((send, send_ref), (keep, keep_ref)):
        out_ref[0] = dot(at_ref[half, :], dg_ref[...]).astype(BF)
        out_ref[1] = dot(at_ref[half, :], du_ref[...]).astype(BF)
        out_ref[2] = dot(byt_ref[half, :], act_ref[...]).astype(BF)


def first_weights(core, at, byt, by, gate, up, wd, layer, start, tiles):
    tile = pl.BlockSpec((T, FT), lambda j, _: (0, start + j))
    out = pl.BlockSpec((3, HALF, FT), lambda j, _: (0, 0, j))
    return pl.pallas_call(
        first_weights_kernel,
        grid_spec=pltpu.PrefetchScalarGridSpec(
            num_scalar_prefetch=1,
            grid=(tiles,),
            in_specs=[
                whole((D, T)),
                whole((D, T)),
                whole((T, D)),
                tile,
                tile,
                pl.BlockSpec((None, FT, D), lambda j, _: (layer, start + j, 0)),
            ],
            out_specs=[out, out],
            scratch_shapes=[pltpu.VMEM((T, FT), BF)] * 3,
        ),
        out_shape=[jax.ShapeDtypeStruct((3, HALF, tiles * FT), BF)] * 2,
        compiler_params=params(),
        cost_estimate=cost(4 * tiles / NT, 80e6 * tiles / NT),
        name="first_weights",
    )(core, at, byt, by, gate, up, wd)


def last_weights_kernel(
    core_ref, at_ref, byt_ref, a2_ref, by2_ref, at2_ref, byt2_ref, act_ref, dg_ref, du_ref, wg_ref, wu_ref, wd_ref,
    keep_ref, send_ref, act2_ref, dg2_ref, du2_ref,
):
    for r in range(NC):
        rows = slice(r * CHUNK, (r + 1) * CHUNK)
        gate = dot(a2_ref[rows, :], wg_ref[...])
        up = dot(a2_ref[rows, :], wu_ref[...])
        by_act = dot_nt(by2_ref[rows, :], wd_ref[...])
        act2_ref[rows, :], dg2_ref[rows, :], du2_ref[rows, :] = gated(gate, up, by_act)
    keep, send = halves(core_ref)
    for half, out_ref in ((send, send_ref), (keep, keep_ref)):
        out_ref[0] = (dot(at_ref[half, :], dg_ref[...]) + dot(at2_ref[half, :], dg2_ref[...])).astype(BF)
        out_ref[1] = (dot(at_ref[half, :], du_ref[...]) + dot(at2_ref[half, :], du2_ref[...])).astype(BF)
        out_ref[2] = (dot(byt_ref[half, :], act_ref[...]) + dot(byt2_ref[half, :], act2_ref[...])).astype(BF)


def last_weights(core, at, byt, a2, by2, at2, byt2, act, dg, du, wg, wu, wd, layer, start, tiles):
    tile = pl.BlockSpec((T, FT), lambda j, _: (0, start + j))
    weight = pl.BlockSpec((None, D, FT), lambda j, _: (layer, 0, start + j))
    out = pl.BlockSpec((3, HALF, FT), lambda j, _: (0, 0, j))
    return pl.pallas_call(
        last_weights_kernel,
        grid_spec=pltpu.PrefetchScalarGridSpec(
            num_scalar_prefetch=1,
            grid=(tiles,),
            in_specs=[
                whole((D, T)), whole((D, T)), whole((T, D)), whole((T, D)), whole((D, T)), whole((D, T)),
                tile, tile, tile, weight, weight,
                pl.BlockSpec((None, FT, D), lambda j, _: (layer, start + j, 0)),
            ],
            out_specs=[out, out],
            scratch_shapes=[pltpu.VMEM((T, FT), BF)] * 3,
        ),
        out_shape=[jax.ShapeDtypeStruct((3, HALF, tiles * FT), BF)] * 2,
        compiler_params=params(),
        cost_estimate=cost(9 * tiles / NT, 90e6 * tiles / NT),
        name="last_weights",
    )(core, at, byt, a2, by2, at2, byt2, act, dg, du, wg, wu, wd)


def adamw(w, m, v, g):
    m = 0.9 * m + 0.1 * g
    v = 0.95 * v + 0.05 * g * g
    step = m * lax.rsqrt(v + 1e-8) + 0.1 * w
    return (w - 0.02 * step).astype(BF), m, v


def adamw_kernel(ranges, n_alias, table_ref, factor_ref, *refs):
    n = len(ranges)
    gradients, refs = refs[:n], refs[n:]
    ins, outs = refs[:9], refs[9 + n_alias :]
    step = pl.program_id(0)
    for g_ref, (first, last) in zip(gradients, ranges, strict=True):

        @pl.when((step >= first) & (step < last))
        def _(g_ref=g_ref):
            factor = factor_ref[0]
            for i in range(3):
                g = g_ref[i].astype(F32) * factor
                if i == 2:
                    g = g.T
                new = adamw(ins[i][...].astype(F32), ins[3 + i][...], ins[6 + i][...], g)
                for which in range(3):
                    outs[3 * which + i][...] = new[which]


def adamw_steps(segments):
    steps = []
    for g, layer, row, start in segments:
        steps += [(layer, row + r, start + f) for r in range(g.shape[1] // ROWS) for f in range(g.shape[2] // FT)]
    return steps


def adamw_blocks(segments, table, begin, factor, arrays, so_far):
    ranges, steps = [], 0
    for g, *_ in segments:
        more = (g.shape[1] // ROWS) * (g.shape[2] // FT)
        ranges.append((steps, steps + more))
        steps += more

    def g_spec(g, start, stop):
        broad = g.shape[2] // FT

        def index(s, *_):
            own = jnp.clip(s - start, 0, stop - start - 1)
            return 0, own // broad, own % broad

        return pl.BlockSpec((3, ROWS, FT), index)

    wide = pl.BlockSpec((None, ROWS, FT), lambda s, t, _: (t[0, s + begin], t[1, s + begin], t[2, s + begin]))
    tall = pl.BlockSpec((None, FT, ROWS), lambda s, t, _: (t[0, s + begin], t[2, s + begin], t[1, s + begin]))
    nine = [wide, wide, tall] * 3
    gradients = [s[0] for s in segments]
    n = len(gradients)
    alias = {2 + n + 9 + i: i for i in range(9)} if so_far else {}
    shapes = [jax.ShapeDtypeStruct(a.shape, BF if i < 3 else F32) for i, a in enumerate(arrays)]
    return pl.pallas_call(
        functools.partial(adamw_kernel, ranges, len(so_far)),
        grid_spec=pltpu.PrefetchScalarGridSpec(
            num_scalar_prefetch=2,
            grid=(steps,),
            in_specs=[g_spec(g, *r) for g, r in zip(gradients, ranges, strict=True)] + nine + [pl.BlockSpec(memory_space=pl.ANY)] * len(so_far),
            out_specs=nine,
        ),
        out_shape=shapes,
        input_output_aliases=alias,
        compiler_params=params(),
        cost_estimate=cost(2.5 * steps / (4 * NT), 190e6 * steps / (4 * NT)),
        name="adamw",
    )(table, factor, *gradients, *arrays, *so_far)


ROWS = QUARTER
FIRST_PARTS = ((0, 6), (6, 5))
LAST_PARTS = ((0, 3), (3, 4), (7, 4))


def solution(mesh):
    def step(x, dy, *arrays):
        wg, wu, wd = arrays[:3]
        me = lax.axis_index("dp")
        chip, core = me >> 1, me & 1
        core_ref = core.astype(jnp.int32).reshape(1)

        def swap_x(a):
            return lax.ppermute(a, "dp", X_SWAP)

        def swap_core(a):
            return lax.ppermute(a, "dp", CORE_SWAP)

        h0, by2 = x[0], dy[0]
        by2_other = swap_x(by2)
        act0, gate0, up0, a0t = gate_up(h0, wg, wu, 0)
        h1, a1, a1t = down(act0, wd, h0, 0)
        h1_other = swap_x(h1)
        act1, dg1, du1 = hidden(a1, by2, wg, wu, wd, 1)
        by1, by1t = states(dg1, du1, wg, wu, h1, by2, 1)
        by2t = turn(by2)

        def piece(g, row):
            return lax.dynamic_slice_in_dim(g, row, QUARTER, 1).astype(F32)

        first = []
        for start, tiles in FIRST_PARTS:
            keep, send = first_weights(core_ref, a0t, by1t, by1, gate0, up0, wd, 0, start, tiles)
            first.append((keep, swap_core(send)))
        partial = []
        for keep, got in first:
            away = (1 - chip) * QUARTER
            away = (piece(keep, away) + piece(got, away)).astype(BF)
            partial.append(swap_x(away))

        a1o, a1ot, by2ot = norm_turn(h1_other, by2_other)
        last = []
        for start, tiles in LAST_PARTS:
            keep, send = last_weights(
                core_ref, a1t, by2t, a1o, by2_other, a1ot, by2ot, act1, dg1, du1, wg, wu, wd, 1, start, tiles,
            )
            last.append((keep, swap_core(send)))

        squares0, squares1 = jnp.zeros((), F32), jnp.zeros((), F32)
        quarters, halves_ = [], []
        for (keep, got), far in zip(first, partial, strict=True):
            mine = (piece(keep, chip * QUARTER) + piece(got, chip * QUARTER) + far.astype(F32)).astype(BF)
            squares0 += jnp.sum(jnp.square(mine.astype(F32)))
            quarters.append(mine)
        for keep, got in last:
            mine = (keep.astype(F32) + got.astype(F32)).astype(BF)
            squares1 += jnp.sum(jnp.square(mine.astype(F32)))
            halves_.append(mine)

        squares0 = squares0.reshape(1, 1)
        squares0 = squares0 + swap_x(squares0)
        squares = squares0 + squares1.reshape(1, 1)
        squares = (squares + swap_core(squares)).reshape(1)
        count = sum(a.size for a in arrays[:3])
        factor = jnp.minimum(1.0, 0.5 * lax.rsqrt(squares / count + 1e-30))

        core_halves = [swap_core(h) for h in halves_]
        far_quarters = [swap_x(q) for q in quarters]
        core_quarters = [swap_core(q) for q in quarters]
        core_far_quarters = [swap_core(q) for q in far_quarters]

        def segments(layer, row, parts, gradients):
            return [(g, layer, row, part[0]) for g, part in zip(gradients, parts, strict=True)]

        groups = [
            segments(1, 0, LAST_PARTS, halves_),
            segments(1, 2, LAST_PARTS, core_halves),
            segments(0, 0, FIRST_PARTS, quarters) + segments(0, 2, FIRST_PARTS, core_quarters),
            segments(0, 1, FIRST_PARTS, far_quarters) + segments(0, 3, FIRST_PARTS, core_far_quarters),
        ]
        steps = [adamw_steps(group) for group in groups]
        table = np.array(sum(steps, []), np.int32).T
        owns = jnp.where(table[0] == 0, 2 * core + chip, 2 * core).astype(jnp.int32)
        table = jnp.asarray(table) ^ (jnp.asarray([[0], [1], [0]], jnp.int32) * owns)
        out, begin = [], 0
        for n, group in enumerate(groups):
            out = adamw_blocks(group, table, begin, factor, arrays, out)
            begin += len(steps[n])
        return tuple(out)

    return jax.shard_map(
        step,
        mesh=mesh,
        in_specs=(P(("rep", "dp"), None, None),) * 2 + (P(None, None, None),) * 9,
        out_specs=(P("rep", None, None),) * 9,
        check_vma=False,
    )
```

time: 1100 us -> 790 us (0.72)
  Pallas kernels: 0 us -> 513 us
  waiting for transfers between devices: 573 us -> 176 us
  matrix products: 325 us -> 0 us
  other arithmetic: 164 us -> 37 us
  starting transfers between devices: 0.04 us -> 46.8 us
  local copies, waits for them, and re-layouts: 13.7 us -> 1.43 us
    psum x1 -> x0, waiting for transfers between devices: 573 us -> none  [step(): summed[number] = [lax.psum(by_w[name], 'dp') for name in NAMES]]
    pallas_call x0 -> x15, Pallas kernels: none -> 513 us  [the longest x4 150 us: adamw_blocks(): pl.pallas_call(functools.partial(adamw_kernel, ranges, len(so_far)), grid...]
    dot_general x15 -> x0, matrix products: 325 us -> none  [the longest x5 114 us: layer(): gate = jnp.dot(a, w['w_gate'], preferred_element_type=jnp.float32)]
    ppermute x0 -> x20, waiting for transfers between devices: none -> 176 us  [the longest x7 176 us: swap_x(): return lax.ppermute(a, 'dp', X_SWAP)]
    convert_element_type x2, other arithmetic: 123 us -> 8.28 us  [step(): away = (piece(keep, away) + piece(got, away)).astype(BF)]
    ppermute x0 -> x20, starting transfers between devices: none -> 46.8 us  [the longest x7 42.5 us: swap_x(): return lax.ppermute(a, 'dp', X_SWAP)]
    unnamed x28 -> x18, local copies, waits for them, and re-layouts: 13.7 us -> 1.43 us
    reduce_sum x4 -> x5, other arithmetic: 34.5 us -> 28.1 us  [the longest x3 17 us: step(): squares1 += jnp.sum(jnp.square(mine.astype(F32)))]
  transfers between devices with their start and end apart: 1 -> 20, of which waited for: 1 -> 6; matrix products, arithmetic and copies ran while one was open for 0% -> 5% of each run, Pallas kernels for 0% -> 40%
where the time goes in v1:
time: 790 us; the launch traced here: 780 us
  Pallas kernels  513 us (65%)
  waiting for transfers between devices  176 us (22%)
  starting transfers between devices  46.8 us (6%)
  other arithmetic  37 us (5%)
    ppermute x7, waiting for transfers between devices, swap_x(): return lax.ppermute(a, 'dp', X_SWAP)  176 us
    pallas_call x4, Pallas kernels, adamw_blocks(): pl.pallas_call(functools.partial(adamw_kernel, ranges, len(so_far)), grid...  150 us
    pallas_call x3, Pallas kernels, last_weights(): pl.pallas_call(last_weights_kernel, grid_spec=pltpu.PrefetchScalarGridSpe...  146 us
    pallas_call x2, Pallas kernels, first_weights(): pl.pallas_call(first_weights_kernel, grid_spec=pltpu.PrefetchScalarGridSp...  66.9 us
    pallas_call x1, Pallas kernels, hidden(): pl.pallas_call(hidden_kernel, grid=(NT,), in_specs=[whole((T, D)), whole(...  45.8 us
    ppermute x7, starting transfers between devices, swap_x(): return lax.ppermute(a, 'dp', X_SWAP)  42.5 us
    pallas_call x1, Pallas kernels, states(): pl.pallas_call(states_kernel, grid=(T // tm,), in_specs=[hidden_rows, hid...  35.4 us
    pallas_call x1, Pallas kernels, gate_up(): pl.pallas_call(gate_up_kernel, grid=(NT,), in_specs=[whole((T, D)), weigh...  34.2 us
  transfers between devices with their start and end apart: 20, of which 6 were waited for; matrix products, arithmetic and copies ran while one was open for 5% of the time, Pallas kernels for 40%

profile of v1, /device:TPU:0, one launch (start us, length us, event | category | flops | bytes accessed | tf_op | source)
XLA Modules:
  0.0 779.9 jit_solution(8947019341046712407)
XLA Ops:
  0.6 34.2 %gate_up.1 = (bf16[2048,2816]{1,0:T(8,128)(2,1)}, f32[2048,2816]{1,0:T(8,128)}, f32[2048,2816]{1,0:T(8,128)}, bf16[1024,2048]{1,0:T(8,128)(2,1)}) custom-call(bf16[2048,1024]{1,0:T(8,128)(2,1)} %bitcast.8, bf16[2,1024,2816]{2,1,0:T(8,128)(2,1)} %refs_4_.7, bf16[2,1024,2816]{2,1,0:T(8,128)(2,1)} %refs_5_.7), custom_call_target="tpu_custom_call" | custom-call | flops 23622320128 | bytes 75000000 | tf_op jit(solution)/shard_map/gate_up/pallas_call | solution.py:70
  34.8 20.5 %down.1 = (bf16[2048,1024]{1,0:T(8,128)(2,1)}, bf16[2048,1024]{1,0:T(8,128)(2,1)}, bf16[1024,2048]{1,0:T(8,128)(2,1)}) custom-call(bf16[2048,2816]{1,0:T(8,128)(2,1)} %get-tuple-element.62.act_ref, bf16[2,2816,1024]{2,1,0:T(8,128)(2,1)} %refs_6_.7, bf16[2048,1024]{1,0:T(8,128)(2,1)} %bitcast.9), custom_call_target="tpu_custom_call" | custom-call | flops 11811160064 | bytes 30000000 | tf_op jit(solution)/shard_map/down/pallas_call | solution.py:98
  55.3 45.8 %hidden.1 = (bf16[2048,2816]{1,0:T(8,128)(2,1)}, bf16[2048,2816]{1,0:T(8,128)(2,1)}, bf16[2048,2816]{1,0:T(8,128)(2,1)}) custom-call(bf16[2048,1024]{1,0:T(8,128)(2,1)} %get-tuple-element.63.a_ref, bf16[2048,1024]{1,0:T(8,128)(2,1)} %bitcast.10, bf16[2,1024,2816]{2,1,0:T(8,128)(2,1)} %refs_4_.7, bf16[2,1024,2816]{2,1,0:T(8,128)(2,1)} %refs_5_.7, ...), custom_call_target="tpu_custom_call" | custom-call | flops 35433480192 | bytes 60000000 | tf_op jit(solution)/shard_map/hidden/pallas_call | solution.py:177
  101.2 35.4 %states.1 = (bf16[2048,1024]{1,0:T(8,128)(2,1)}, bf16[1024,2048]{1,0:T(8,128)(2,1)}) custom-call(bf16[2048,2816]{1,0:T(8,128)(2,1)} %get-tuple-element.64.dg_ref, bf16[2048,2816]{1,0:T(8,128)(2,1)} %get-tuple-element.65.du_ref, bf16[2,1024,2816]{2,1,0:T(8,128)(2,1)} %refs_4_.7, bf16[2,1024,2816]{2,1,0:T(8,128)(2,1)} %refs_5_.7, ...), custom_call_target="tpu_custom_call" | custom-call | flops 23622320128 | bytes 45000000 | tf_op jit(solution)/shard_map/states/pallas_call | solution.py:206
  136.6 31.1 %first_weights.3 = (bf16[3,512,1280]{2,1,0:T(8,128)(2,1)}, bf16[3,512,1280]{2,1,0:T(8,128)(2,1)}) custom-call(s32[1]{0:T(128)} %bitcast.core_ref, bf16[1024,2048]{1,0:T(8,128)(2,1)} %get-tuple-element.61.at_ref, bf16[1024,2048]{1,0:T(8,128)(2,1)} %get-tuple-element.67.byt_ref, bf16[2048,1024]{1,0:T(8,128)(2,1)} %get-tuple-element.68.by_ref, ...), custom_call_target="tpu_custom_call" | custom-call | flops 21474836480 | bytes 36363636 | tf_op jit(solution)/shard_map/first_weights/pallas_call | solution.py:239
  167.7 0.8 collective-permute-start.2
  168.5 2.5 collective-permute-start.5
  171.0 0.0 collective-permute-start.6
  171.1 35.8 %first_weights.2 = (bf16[3,512,1536]{2,1,0:T(8,128)(2,1)}, bf16[3,512,1536]{2,1,0:T(8,128)(2,1)}) custom-call(s32[1]{0:T(128)} %bitcast.core_ref, bf16[1024,2048]{1,0:T(8,128)(2,1)} %get-tuple-element.61.at_ref, bf16[1024,2048]{1,0:T(8,128)(2,1)} %get-tuple-element.67.byt_ref, bf16[2048,1024]{1,0:T(8,128)(2,1)} %get-tuple-element.68.by_ref, ...), custom_call_target="tpu_custom_call" | custom-call | flops 25769803776 | bytes 43636364 | tf_op jit(solution)/shard_map/first_weights/pallas_call | solution.py:239
  206.8 0.2 collective-permute-start
  207.0 5.2 turn.1.byt_ref
  212.2 0.0 collective-permute-done.2
  212.2 3.9 add_convert_fusion.6
  216.1 1.8 collective-permute-start.3
  217.9 44.8 %collective-permute-done.5.h_ref = bf16[2048,1024]{1,0:T(8,128)(2,1)} collective-permute-done((bf16[2048,1024]{1,0:T(8,128)(2,1)}, bf16[2048,1024]{1,0:T(8,128)(2,1)}, u32[]{:S(2)}, u32[]{:S(2)}) %collective-permute-start.5) | collective-permute-done | bytes 4194336 | tf_op jit(solution)/shard_map/ppermute | solution.py:388
  262.8 89.9 %collective-permute-done.6.x_ref.by2_ref = bf16[2048,1024]{1,0:T(8,128)(2,1)} collective-permute-done((bf16[2048,1024]{1,0:T(8,128)(2,1)}, bf16[2048,1024]{1,0:T(8,128)(2,1)}, u32[]{:S(2)}, u32[]{:S(2)}) %collective-permute-start.6) | collective-permute-done | bytes 4194336 | tf_op jit(solution)/shard_map/ppermute | solution.py:388
  352.7 9.1 %norm_turn.1 = (bf16[2048,1024]{1,0:T(8,128)(2,1)}, bf16[1024,2048]{1,0:T(8,128)(2,1)}, bf16[1024,2048]{1,0:T(8,128)(2,1)}) custom-call(bf16[2048,1024]{1,0:T(8,128)(2,1)} %collective-permute-done.5.h_ref, bf16[2048,1024]{1,0:T(8,128)(2,1)} %collective-permute-done.6.x_ref.by2_ref), custom_call_target="tpu_custom_call" | custom-call | flops 4724464128 | bytes 20000000 | tf_op jit(solution)/shard_map/norm_turn/pallas_call | solution.py:145
  361.7 51.7 %last_weights.5 = (bf16[3,512,1024]{2,1,0:T(8,128)(2,1)}, bf16[3,512,1024]{2,1,0:T(8,128)(2,1)}) custom-call(s32[1]{0:T(128)} %bitcast.core_ref, bf16[1024,2048]{1,0:T(8,128)(2,1)} %get-tuple-element.75.at_ref, bf16[1024,2048]{1,0:T(8,128)(2,1)} %turn.1.byt_ref, bf16[2048,1024]{1,0:T(8,128)(2,1)} %get-tuple-element.76.a2_ref, ...), custom_call_target="tpu_custom_call" | custom-call | flops 38654705664 | bytes 32727272 | tf_op jit(solution)/shard_map/last_weights/pallas_call | solution.py:283
  413.4 0.0 collective-permute-start.9
  413.5 41.7 %last_weights.3 = (bf16[3,512,768]{2,1,0:T(8,128)(2,1)}, bf16[3,512,768]{2,1,0:T(8,128)(2,1)}) custom-call(s32[1]{0:T(128)} %bitcast.core_ref, bf16[1024,2048]{1,0:T(8,128)(2,1)} %get-tuple-element.75.at_ref, bf16[1024,2048]{1,0:T(8,128)(2,1)} %turn.1.byt_ref, bf16[2048,1024]{1,0:T(8,128)(2,1)} %get-tuple-element.76.a2_ref, ...), custom_call_target="tpu_custom_call" | custom-call | flops 28991029248 | bytes 24545454 | tf_op jit(solution)/shard_map/last_weights/pallas_call | solution.py:283
  455.2 0.5 collective-permute-start.7
  455.7 52.3 %last_weights.4 = (bf16[3,512,1024]{2,1,0:T(8,128)(2,1)}, bf16[3,512,1024]{2,1,0:T(8,128)(2,1)}) custom-call(s32[1]{0:T(128)} %bitcast.core_ref, bf16[1024,2048]{1,0:T(8,128)(2,1)} %get-tuple-element.75.at_ref, bf16[1024,2048]{1,0:T(8,128)(2,1)} %turn.1.byt_ref, bf16[2048,1024]{1,0:T(8,128)(2,1)} %get-tuple-element.76.a2_ref, ...), custom_call_target="tpu_custom_call" | custom-call | flops 38654705664 | bytes 32727272 | tf_op jit(solution)/shard_map/last_weights/pallas_call | solution.py:283
  508.0 0.1 collective-permute-start.8
  508.1 0.0 collective-permute-done
  508.1 4.4 add_convert_fusion.4
  512.5 2.0 collective-permute-start.1
  514.5 0.0 collective-permute-done.3
  514.5 5.6 multiply_reduce_fusion.4
  520.1 0.0 collective-permute-start.12
  520.1 0.0 collective-permute-done.7
  520.1 1.4 copy-done.3
  521.5 4.6 multiply_reduce_fusion.2
  526.1 0.2 collective-permute-start.17
  526.3 0.0 collective-permute-done.9
  526.3 6.5 multiply_reduce_fusion
  532.8 0.2 collective-permute-start.19
  533.0 0.0 collective-permute-done.8
  533.0 5.9 multiply_reduce_fusion.1
  538.9 0.3 collective-permute-start.18
  539.2 27.7 %collective-permute-done.1 = bf16[3,256,1536]{2,1,0:T(8,128)(2,1)} collective-permute-done((bf16[3,256,1536]{2,1,0:T(8,128)(2,1)}, bf16[3,256,1536]{2,1,0:T(8,128)(2,1)}, u32[]{:S(2)}, u32[]{:S(2)}) %collective-permute-start.1) | collective-permute-done | bytes 2359328 | tf_op jit(solution)/shard_map/ppermute | solution.py:388
  566.9 5.5 multiply_reduce_fusion.3
  573.7 34.4 %collective-permute-start.4 = (f32[1,1]{1,0:T(1,128)}, f32[1,1]{1,0:T(1,128)}, u32[]{:S(2)}, u32[]{:S(2)}) collective-permute-start(f32[1,1]{1,0:T(1,128)} %bitcast.3), channel_id=1, source_target_pairs={{0,2},{2,0},{1,3},{3,1},{4,6},{6,4},{5,7},{7,5}} | collective-permute-start | bytes 20 | tf_op jit(solution)/shard_map/ppermute | solution.py:388
  608.1 0.7 collective-permute-done.4
  611.5 1.0 collective-permute-start.10
  612.5 0.3 collective-permute-done.10
  612.8 1.7 collective-permute-start.11
  614.6 0.6 multiply_xor_fusion.table_ref
  615.9 0.0 collective-permute-done.12.refs_1_
  615.9 0.0 collective-permute-start.16
  615.9 0.0 collective-permute-done.17.refs_0_
  615.9 0.5 collective-permute-start.15
  616.4 37.5 %adamw.4 = (bf16[2,1024,2816]{2,1,0:T(8,128)(2,1)}, bf16[2,1024,2816]{2,1,0:T(8,128)(2,1)}, bf16[2,2816,1024]{2,1,0:T(8,128)(2,1)}, f32[2,1024,2816]{2,1,0:T(8,1...) custom-call(s32[3,88]{1,0:T(4,128)} %multiply_xor_fusion.table_ref, ...), custom_call_target="tpu_custom_call" | custom-call | flops 14763950080 | bytes 95000000 | tf_op jit(solution)/shard_map/adamw/pallas_call | solution.py:359
  653.9 12.5 %collective-permute-done.11.refs_0_ = bf16[3,256,1536]{2,1,0:T(8,128)(2,1)} collective-permute-done((bf16[3,256,1536]{2,1,0:T(8,128)(2,1)}, bf16[3,256,1536]{2,1,0:T(8,128)(2,1)}, u32[]{:S(2)}, u32[]{:S(2)}) %collective-permute-start.11) | collective-permute-done | bytes 2359328 | tf_op jit(solution)/shard_map/ppermute | solution.py:388
  666.4 0.0 collective-permute-start.14
  666.4 0.0 collective-permute-done.19.refs_2_
  666.4 0.5 collective-permute-start.13
  666.9 0.0 collective-permute-done.18.refs_1_
  666.9 37.7 %adamw.5 = (bf16[2,1024,2816]{2,1,0:T(8,128)(2,1)}, bf16[2,1024,2816]{2,1,0:T(8,128)(2,1)}, bf16[2,2816,1024]{2,1,0:T(8,128)(2,1)}, f32[2,1024,2816]{2,1,0:T(8,1...) custom-call(s32[3,88]{1,0:T(4,128)} %multiply_xor_fusion.table_ref, ...), custom_call_target="tpu_custom_call", output_to_operand_aliasing={{0}: (14, {}), {1}: (15, {}), {2}: (16, {}), {3}: (17, {}),... | custom-call | flops 14763950080 | bytes 95000000 | tf_op jit(solution)/shard_map/adamw/pallas_call | solution.py:359
  704.6 0.0 collective-permute-done.16.refs_3_
  704.6 0.0 collective-permute-done.15.refs_2_
  704.6 37.5 %adamw.6 = (bf16[2,1024,2816]{2,1,0:T(8,128)(2,1)}, bf16[2,1024,2816]{2,1,0:T(8,128)(2,1)}, bf16[2,2816,1024]{2,1,0:T(8,128)(2,1)}, f32[2,1024,2816]{2,1,0:T(8,1...) custom-call(s32[3,88]{1,0:T(4,128)} %multiply_xor_fusion.table_ref, ...), custom_call_target="tpu_custom_call", output_to_operand_aliasing={{0}: (15, {}), {1}: (16, {}), {2}: (17, {}), {3}: (18, {}),... | custom-call | flops 14763950080 | bytes 95000000 | tf_op jit(solution)/shard_map/adamw/pallas_call | solution.py:359
  742.1 0.0 collective-permute-done.14.refs_3_
  742.2 0.0 collective-permute-done.13.refs_2_
  742.2 37.5 %adamw.7 = (bf16[2,1024,2816]{2,1,0:T(8,128)(2,1)}, bf16[2,1024,2816]{2,1,0:T(8,128)(2,1)}, bf16[2,2816,1024]{2,1,0:T(8,128)(2,1)}, f32[2,1024,2816]{2,1,0:T(8,1...) custom-call(s32[3,88]{1,0:T(4,128)} %multiply_xor_fusion.table_ref, ...), custom_call_target="tpu_custom_call", output_to_operand_aliasing={{0}: (15, {}), {1}: (16, {}), {2}: (17, {}), {3}: (18, {}),... | custom-call | flops 14763950080 | bytes 95000000 | tf_op jit(solution)/shard_map/adamw/pallas_call | solution.py:359
  (19 shorter events, 0.0 us)
Async XLA Ops:
  167.7 44.5 %collective-permute-start.2 = (bf16[3,512,1280]{2,1,0:T(8,128)(2,1)}, bf16[3,512,1280]{2,1,0:T(8,128)(2,1)}, u32[]{:S(2)}, u32[]{:S(2)}) collective-permute-start(bf16[3,512,1280]{2,1,0:T(8,128)(2,1)} %get-tuple-element.74), channel_id=1, source_target_pairs={{0,1},{1,0},{2,3},{3,2},{4,5},{5,4},{6,7},{7,6}} | collective-permute-start | bytes 11796488 | tf_op jit(solution)/shard_map/ppermute | solution.py:391
  168.5 94.2 %collective-permute-start.5 = (bf16[2048,1024]{1,0:T(8,128)(2,1)}, bf16[2048,1024]{1,0:T(8,128)(2,1)}, u32[]{:S(2)}, u32[]{:S(2)}) collective-permute-start(bf16[2048,1024]{1,0:T(8,128)(2,1)} %get-tuple-element.66.h_ref), channel_id=1, source_target_pairs={{0,2},{2,0},{1,3},{3,1},{4,6},{6,4},{5,7},{7,5}} | collective-permute-start | bytes 12582920 | tf_op jit(solution)/shard_map/ppermute | solution.py:388
  171.0 181.6 %collective-permute-start.6 = (bf16[2048,1024]{1,0:T(8,128)(2,1)}, bf16[2048,1024]{1,0:T(8,128)(2,1)}, u32[]{:S(2)}, u32[]{:S(2)}) collective-permute-start(bf16[2048,1024]{1,0:T(8,128)(2,1)} %bitcast.12), channel_id=1, source_target_pairs={{0,2},{2,0},{1,3},{3,1},{4,6},{6,4},{5,7},{7,5}} | collective-permute-start | bytes 12582920 | tf_op jit(solution)/shard_map/ppermute | solution.py:388
  206.8 301.2 %collective-permute-start = (bf16[3,512,1536]{2,1,0:T(8,128)(2,1)}, bf16[3,512,1536]{2,1,0:T(8,128)(2,1)}, u32[]{:S(2)}, u32[]{:S(2)}) collective-permute-start(bf16[3,512,1536]{2,1,0:T(8,128)(2,1)} %get-tuple-element.72), channel_id=1, source_target_pairs={{0,1},{1,0},{2,3},{3,2},{4,5},{5,4},{6,7},{7,6}} | collective-permute-start | bytes 14155784 | tf_op jit(solution)/shard_map/ppermute | solution.py:391
  216.1 298.4 %collective-permute-start.3 = (bf16[3,256,1280]{2,1,0:T(8,128)(2,1)}, bf16[3,256,1280]{2,1,0:T(8,128)(2,1)}, u32[]{:S(2)}, u32[]{:S(2)}) collective-permute-start(bf16[3,256,1280]{2,1,0:T(8,128)(2,1)} %add_convert_fusion.6), channel_id=1, source_target_pairs={{0,2},{2,0},{1,3},{3,1},{4,6},{6,4},{5,7},{7,5}} | collective-permute-start | bytes 5898248 | tf_op jit(solution)/shard_map/ppermute | solution.py:388
  413.4 112.8 %collective-permute-start.9 = (bf16[3,512,1024]{2,1,0:T(8,128)(2,1)}, bf16[3,512,1024]{2,1,0:T(8,128)(2,1)}, u32[]{:S(2)}, u32[]{:S(2)}) collective-permute-start(bf16[3,512,1024]{2,1,0:T(8,128)(2,1)} %get-tuple-element.85), channel_id=1, source_target_pairs={{0,1},{1,0},{2,3},{3,2},{4,5},{5,4},{6,7},{7,6}} | collective-permute-start | bytes 9437192 | tf_op jit(solution)/shard_map/ppermute | solution.py:391
  455.2 64.9 %collective-permute-start.7 = (bf16[3,512,768]{2,1,0:T(8,128)(2,1)}, bf16[3,512,768]{2,1,0:T(8,128)(2,1)S(1)}, u32[]{:S(2)}, u32[]{:S(2)}) collective-permute-start(bf16[3,512,768]{2,1,0:T(8,128)(2,1)} %get-tuple-element.81), channel_id=1, source_target_pairs={{0,1},{1,0},{2,3},{3,2},{4,5},{5,4},{6,7},{7,6}} | collective-permute-start | bytes 7077896 | tf_op jit(solution)/shard_map/ppermute | solution.py:391
  508.0 25.0 %collective-permute-start.8 = (bf16[3,512,1024]{2,1,0:T(8,128)(2,1)}, bf16[3,512,1024]{2,1,0:T(8,128)(2,1)}, u32[]{:S(2)}, u32[]{:S(2)}) collective-permute-start(bf16[3,512,1024]{2,1,0:T(8,128)(2,1)} %get-tuple-element.83), channel_id=1, source_target_pairs={{0,1},{1,0},{2,3},{3,2},{4,5},{5,4},{6,7},{7,6}} | collective-permute-start | bytes 9437192 | tf_op jit(solution)/shard_map/ppermute | solution.py:391
  512.5 54.4 %collective-permute-start.1 = (bf16[3,256,1536]{2,1,0:T(8,128)(2,1)}, bf16[3,256,1536]{2,1,0:T(8,128)(2,1)}, u32[]{:S(2)}, u32[]{:S(2)}) collective-permute-start(bf16[3,256,1536]{2,1,0:T(8,128)(2,1)} %add_convert_fusion.4), channel_id=1, source_target_pairs={{0,2},{2,0},{1,3},{3,1},{4,6},{6,4},{5,7},{7,5}} | collective-permute-start | bytes 7077896 | tf_op jit(solution)/shard_map/ppermute | solution.py:388
  520.1 6.2 copy-start.1
  520.1 95.8 %collective-permute-start.12 = (bf16[3,256,1280]{2,1,0:T(8,128)(2,1)}, bf16[3,256,1280]{2,1,0:T(8,128)(2,1)}, u32[]{:S(2)}, u32[]{:S(2)}) collective-permute-start(bf16[3,256,1280]{2,1,0:T(8,128)(2,1)} %get-tuple-element.120.refs_1_), channel_id=1, source_target_pairs={{0,2},{2,0},{1,3},{3,1},{4,6},{6,4},{5,7},{7,5}} | collective-permute-start | bytes 5898248 | tf_op jit(solution)/shard_map/ppermute | solution.py:388
  520.1 1.4 copy-start.3
  526.1 6.7 copy-start
  526.1 89.8 %collective-permute-start.17 = (bf16[3,512,768]{2,1,0:T(8,128)(2,1)S(1)}, bf16[3,512,768]{2,1,0:T(8,128)(2,1)}, u32[]{:S(2)}, u32[]{:S(2)}) collective-permute-start(bf16[3,512,768]{2,1,0:T(8,128)(2,1)S(1)} %get-tuple-element.118.refs_0_), channel_id=1, source_target_pairs={{0,1},{1,0},{2,3},{3,2},{4,5},{5,4},{6,7},{7,6}} | collective-permute-start | bytes 7077896 | tf_op jit(solution)/shard_map/ppermute | solution.py:391
  526.3 6.7 copy-start.2
  526.3 40.6 %slice-start = ((s8[4718592]{0:T(1024)(128)(4,1)}), s8[4194304]{0:T(1024)(128)(4,1)S(1)}, s32[]{:S(2)}) async-start(s8[4718592]{0:T(1024)(128)(4,1)} %bitcast.6), calls=%async_computation | async-start | bytes 8388608
  532.8 34.1 %slice-start.1 = ((s8[4718592]{0:T(1024)(128)(4,1)}), s8[524288]{0:T(1024)(128)(4,1)S(1)}, s32[]{:S(2)}) async-start(s8[4718592]{0:T(1024)(128)(4,1)} %bitcast.6), calls=%async_computation.1 | async-start | bytes 1048576
  532.8 133.6 %collective-permute-start.19 = (bf16[3,512,1024]{2,1,0:T(8,128)(2,1)}, bf16[3,512,1024]{2,1,0:T(8,128)(2,1)}, u32[]{:S(2)}, u32[]{:S(2)}) collective-permute-start(bf16[3,512,1024]{2,1,0:T(8,128)(2,1)} %get-tuple-element.114.refs_2_), channel_id=1, source_target_pairs={{0,1},{1,0},{2,3},{3,2},{4,5},{5,4},{6,7},{7,6}} | collective-permute-start | bytes 9437192 | tf_op jit(solution)/shard_map/ppermute | solution.py:391
  538.9 75.6 %copy-start.6 = (pred[88]{0:T(512)(128)(4,1)S(1)}, pred[88]{0:T(512)(128)(4,1)}, u32[]{:S(2)}) copy-start(pred[88]{0:T(512)(128)(4,1)} %constant.34.clone) | copy-start | bytes 268
  538.9 75.6 %copy-start.4 = (s32[3,88]{1,0:T(4,128)S(1)}, s32[3,88]{1,0:T(4,128)}, u32[]{:S(2)}) copy-start(s32[3,88]{1,0:T(4,128)} %constant.35.clone) | copy-start | bytes 3172
  538.9 75.6 %copy-start.5 = (s32[3]{0:T(128)S(1)}, s32[3]{0:T(128)}, u32[]{:S(2)}) copy-start(s32[3]{0:T(128)} %constant.39) | copy-start | bytes 40
  538.9 128.0 %collective-permute-start.18 = (bf16[3,512,1024]{2,1,0:T(8,128)(2,1)}, bf16[3,512,1024]{2,1,0:T(8,128)(2,1)}, u32[]{:S(2)}, u32[]{:S(2)}) collective-permute-start(bf16[3,512,1024]{2,1,0:T(8,128)(2,1)} %get-tuple-element.116.refs_1_), channel_id=1, source_target_pairs={{0,1},{1,0},{2,3},{3,2},{4,5},{5,4},{6,7},{7,6}} | collective-permute-start | bytes 9437192 | tf_op jit(solution)/shard_map/ppermute | solution.py:391
  573.7 35.1 %collective-permute-start.4 = (f32[1,1]{1,0:T(1,128)}, f32[1,1]{1,0:T(1,128)}, u32[]{:S(2)}, u32[]{:S(2)}) collective-permute-start(f32[1,1]{1,0:T(1,128)} %bitcast.3), channel_id=1, source_target_pairs={{0,2},{2,0},{1,3},{3,1},{4,6},{6,4},{5,7},{7,5}} | collective-permute-start | bytes 20 | tf_op jit(solution)/shard_map/ppermute | solution.py:388
  611.5 1.3 collective-permute-start.10
  612.8 53.6 %collective-permute-start.11 = (bf16[3,256,1536]{2,1,0:T(8,128)(2,1)}, bf16[3,256,1536]{2,1,0:T(8,128)(2,1)}, u32[]{:S(2)}, u32[]{:S(2)}) collective-permute-start(bf16[3,256,1536]{2,1,0:T(8,128)(2,1)} %get-tuple-element.122.refs_0_), channel_id=1, source_target_pairs={{0,2},{2,0},{1,3},{3,1},{4,6},{6,4},{5,7},{7,5}} | collective-permute-start | bytes 7077896 | tf_op jit(solution)/shard_map/ppermute | solution.py:388
  615.9 88.7 %collective-permute-start.16 = (bf16[3,256,1280]{2,1,0:T(8,128)(2,1)}, bf16[3,256,1280]{2,1,0:T(8,128)(2,1)}, u32[]{:S(2)}, u32[]{:S(2)}) collective-permute-start(bf16[3,256,1280]{2,1,0:T(8,128)(2,1)} %get-tuple-element.120.refs_1_), channel_id=1, source_target_pairs={{0,1},{1,0},{2,3},{3,2},{4,5},{5,4},{6,7},{7,6}} | collective-permute-start | bytes 5898248 | tf_op jit(solution)/shard_map/ppermute | solution.py:391
  615.9 88.7 %collective-permute-start.15 = (bf16[3,256,1536]{2,1,0:T(8,128)(2,1)}, bf16[3,256,1536]{2,1,0:T(8,128)(2,1)}, u32[]{:S(2)}, u32[]{:S(2)}) collective-permute-start(bf16[3,256,1536]{2,1,0:T(8,128)(2,1)} %get-tuple-element.122.refs_0_), channel_id=1, source_target_pairs={{0,1},{1,0},{2,3},{3,2},{4,5},{5,4},{6,7},{7,6}} | collective-permute-start | bytes 7077896 | tf_op jit(solution)/shard_map/ppermute | solution.py:391
  666.4 75.7 %collective-permute-start.14 = (bf16[3,256,1280]{2,1,0:T(8,128)(2,1)}, bf16[3,256,1280]{2,1,0:T(8,128)(2,1)}, u32[]{:S(2)}, u32[]{:S(2)}) collective-permute-start(bf16[3,256,1280]{2,1,0:T(8,128)(2,1)} %collective-permute-done.12.refs_1_), channel_id=1, source_target_pairs={{0,1},{1,0},{2,3},{3,2},{4,5},{5,4},{6,7},{7,6}} | collective-permute-start | bytes 5898248 | tf_op jit(solution)/shard_map/ppermute | solution.py:391
  666.4 75.7 %collective-permute-start.13 = (bf16[3,256,1536]{2,1,0:T(8,128)(2,1)}, bf16[3,256,1536]{2,1,0:T(8,128)(2,1)}, u32[]{:S(2)}, u32[]{:S(2)}) collective-permute-start(bf16[3,256,1536]{2,1,0:T(8,128)(2,1)} %collective-permute-done.11.refs_0_), channel_id=1, source_target_pairs={{0,1},{1,0},{2,3},{3,2},{4,5},{5,4},{6,7},{7,6}} | collective-permute-start | bytes 7077896 | tf_op jit(solution)/shard_map/ppermute | solution.py:391

commit v2 on v1

v2 whole, which is shorter than its diff:
```python
import functools

import jax
import jax.numpy as jnp
import numpy as np
from jax import lax
from jax.experimental import pallas as pl
from jax.experimental.pallas import tpu as pltpu
from jax.sharding import PartitionSpec as P

BF, F32 = jnp.bfloat16, jnp.float32
T, D, FF = 2048, 1024, 2816
FT = 256
NT = FF // FT
HALF, QUARTER = D // 2, D // 4
CHUNK = 512
NC = T // CHUNK
ROWS, BROAD, SOME, UNROLL = QUARTER, FF // 2, 16, 2
TURN = 256
X_SWAP = [(0, 2), (2, 0), (1, 3), (3, 1)]
CORE_SWAP = [(0, 1), (1, 0), (2, 3), (3, 2)]
VMEM_LIMIT = 64 * 1000 * 1000
EPS = 1e-6


def dot(a, b):
    return jnp.dot(a, b, preferred_element_type=F32)


def dot_nt(a, b):
    return lax.dot_general(a, b, (((1,), (1,)), ((), ())), preferred_element_type=F32)


def params(**more):
    if more:
        more["has_side_effects"] = True
    return pltpu.CompilerParams(dimension_semantics=("arbitrary",), vmem_limit_bytes=VMEM_LIMIT, **more)


def cost(matmuls, nbytes):
    return pl.CostEstimate(flops=int(matmuls * 2 * T * D * FF), bytes_accessed=int(nbytes), transcendentals=0)


def norm(h):
    wide = h.astype(F32)
    return wide * lax.rsqrt(jnp.mean(wide * wide, -1, keepdims=True) + EPS)


def whole(shape):
    return pl.BlockSpec(shape, lambda *_: (0,) * len(shape))


def gate_up_kernel(h_ref, wg_ref, wu_ref, act_ref, gate_ref, up_ref, at_ref, a_ref):
    @pl.when(pl.program_id(0) == 0)
    def _():
        for r in range(NC):
            rows = slice(r * CHUNK, (r + 1) * CHUNK)
            a = norm(h_ref[rows, :]).astype(BF)
            a_ref[rows, :] = a
            at_ref[:, rows] = a.T

    for r in range(NC):
        rows = slice(r * CHUNK, (r + 1) * CHUNK)
        gate = dot(a_ref[rows, :], wg_ref[...])
        up = dot(a_ref[rows, :], wu_ref[...])
        gate_ref[rows, :] = gate
        up_ref[rows, :] = up
        act_ref[rows, :] = (gate * jax.nn.sigmoid(gate) * up).astype(BF)


def gate_up(h, wg, wu, layer):
    weight = pl.BlockSpec((None, D, FT), lambda j: (layer, 0, j))
    tile = pl.BlockSpec((T, FT), lambda j: (0, j))
    return pl.pallas_call(
        gate_up_kernel,
        grid=(NT,),
        in_specs=[whole((T, D)), weight, weight],
        out_specs=[tile, tile, tile, whole((D, T))],
        out_shape=[
            jax.ShapeDtypeStruct((T, FF), BF),
            jax.ShapeDtypeStruct((T, FF), F32),
            jax.ShapeDtypeStruct((T, FF), F32),
            jax.ShapeDtypeStruct((D, T), BF),
        ],
        scratch_shapes=[pltpu.VMEM((T, D), BF)],
        compiler_params=params(),
        cost_estimate=cost(2, 75e6),
        name="gate_up",
    )(h, wg, wu)


def down_kernel(act_ref, w_ref, h_ref, out_ref, a_ref, at_ref):
    h = h_ref[...] + dot(act_ref[...], w_ref[...]).astype(BF)
    out_ref[...] = h
    a = norm(h).astype(BF)
    a_ref[...] = a
    at_ref[...] = a.T


def down(act, w, h, layer):
    rows = pl.BlockSpec((CHUNK, D), lambda i: (i, 0))
    return pl.pallas_call(
        down_kernel,
        grid=(NC,),
        in_specs=[
            pl.BlockSpec((CHUNK, FF), lambda i: (i, 0)),
            pl.BlockSpec((None, FF, D), lambda i: (layer, 0, 0)),
            rows,
        ],
        out_specs=[rows, rows, pl.BlockSpec((D, CHUNK), lambda i: (0, i))],
        out_shape=[
            jax.ShapeDtypeStruct((T, D), BF),
            jax.ShapeDtypeStruct((T, D), BF),
            jax.ShapeDtypeStruct((D, T), BF),
        ],
        compiler_params=params(),
        cost_estimate=cost(1, 30e6),
        name="down",
    )(act, w, h)


def norm_turn_kernel(h_ref, x_ref, a_ref, at_ref, xt_ref):
    a = norm(h_ref[...]).astype(BF)
    a_ref[...] = a
    at_ref[...] = a.T
    xt_ref[...] = x_ref[...].T


def norm_turn(h, x):
    rows = pl.BlockSpec((CHUNK, D), lambda i: (i, 0))
    columns = pl.BlockSpec((D, CHUNK), lambda i: (0, i))
    return pl.pallas_call(
        norm_turn_kernel,
        grid=(NC,),
        in_specs=[rows, rows],
        out_specs=[rows, columns, columns],
        out_shape=[jax.ShapeDtypeStruct((T, D), BF), jax.ShapeDtypeStruct((D, T), BF), jax.ShapeDtypeStruct((D, T), BF)],
        compiler_params=params(),
        cost_estimate=cost(0.4, 20e6),
        name="norm_turn",
    )(h, x)


def gated(gate, up, by_act):
    by_act = by_act.astype(BF).astype(F32)
    sig = jax.nn.sigmoid(gate)
    silu = gate * sig
    by_gate = by_act * up * (sig + silu * (1.0 - sig))
    return (silu * up).astype(BF), by_gate.astype(BF), (by_act * silu).astype(BF)


def hidden_kernel(a_ref, by_ref, wg_ref, wu_ref, wd_ref, act_ref, dg_ref, du_ref, byt_ref):
    turned = jnp.minimum(pl.program_id(0), T // TURN - 1)
    byt_ref[...] = by_ref[pl.ds(pl.multiple_of(turned * TURN, TURN), TURN), :].T
    for r in range(NC):
        rows = slice(r * CHUNK, (r + 1) * CHUNK)
        gate = dot(a_ref[rows, :], wg_ref[...])
        up = dot(a_ref[rows, :], wu_ref[...])
        by_act = dot_nt(by_ref[rows, :], wd_ref[...])
        act_ref[rows, :], dg_ref[rows, :], du_ref[rows, :] = gated(gate, up, by_act)


def hidden(a, by, wg, wu, wd, layer):
    weight = pl.BlockSpec((None, D, FT), lambda j: (layer, 0, j))
    tile = pl.BlockSpec((T, FT), lambda j: (0, j))
    return pl.pallas_call(
        hidden_kernel,
        grid=(NT,),
        in_specs=[whole((T, D)), whole((T, D)), weight, weight, pl.BlockSpec((None, FT, D), lambda j: (layer, j, 0))],
        out_specs=[tile, tile, tile, pl.BlockSpec((D, TURN), lambda j: (0, jnp.minimum(j, T // TURN - 1)))],
        out_shape=[jax.ShapeDtypeStruct((T, FF), BF)] * 3 + [jax.ShapeDtypeStruct((D, T), BF)],
        compiler_params=params(),
        cost_estimate=cost(3, 60e6),
        name="hidden",
    )(a, by, wg, wu, wd)


def states_kernel(dg_ref, du_ref, wg_ref, wu_ref, h_ref, by_ref, out_ref, outt_ref):
    by_a = dot_nt(dg_ref[...], wg_ref[...]).astype(BF) + dot_nt(du_ref[...], wu_ref[...]).astype(BF)
    wide = h_ref[...].astype(F32)
    by_a = by_a.astype(F32)
    scale = lax.rsqrt(jnp.mean(wide * wide, -1, keepdims=True) + EPS)
    inner = jnp.mean(by_a * wide, -1, keepdims=True)
    by_h = by_a * scale - wide * (inner * scale * scale * scale)
    out = by_ref[...] + by_h.astype(BF)
    out_ref[...] = out
    outt_ref[...] = out.T


def states(dg, du, wg, wu, h, by, layer):
    tm = 256
    rows = pl.BlockSpec((tm, D), lambda i: (i, 0))
    hidden_rows = pl.BlockSpec((tm, FF), lambda i: (i, 0))
    weight = pl.BlockSpec((None, D, FF), lambda i: (layer, 0, 0))
    return pl.pallas_call(
        states_kernel,
        grid=(T // tm,),
        in_specs=[hidden_rows, hidden_rows, weight, weight, rows, rows],
        out_specs=[rows, pl.BlockSpec((D, tm), lambda i: (0, i))],
        out_shape=[jax.ShapeDtypeStruct((T, D), BF), jax.ShapeDtypeStruct((D, T), BF)],
        compiler_params=params(),
        cost_estimate=cost(2, 45e6),
        name="states",
    )(dg, du, wg, wu, h, by)


def positions():
    me = lax.axis_index("dp")
    return lax.div(me, 2), lax.rem(me, 2), me + 1 - 2 * lax.rem(me, 2)


def part(index, size):
    return pl.ds(pl.multiple_of(index * size, size), size)


class Exchange:
    scratch = (
        pltpu.VMEM((2, 3, HALF, FT), BF),
        pltpu.VMEM((3, 3, HALF, FT), F32),
        pltpu.VMEM((NT, 3, HALF, FT), BF),
        pltpu.SemaphoreType.DMA((NT,)),
        pltpu.SemaphoreType.DMA((NT,)),
    )

    def __init__(self, sent, kept, got, send_sem, got_sem):
        self.sent, self.kept, self.got = sent, kept, got
        self.send_sem, self.got_sem = send_sem, got_sem
        self.chip, self.core, self.other = positions()

    def greet(self):
        barrier = pltpu.get_barrier_semaphore()
        pl.semaphore_signal(barrier, inc=1, device_id={"dp": self.other}, device_id_type=pl.DeviceIdType.MESH)
        pl.semaphore_wait(barrier, 1)

    def copy(self, j):
        return pltpu.make_async_remote_copy(
            src_ref=self.sent.at[lax.rem(j, 2)],
            dst_ref=self.got.at[j],
            send_sem=self.send_sem.at[j],
            recv_sem=self.got_sem.at[j],
            device_id={"dp": self.other},
            device_id_type=pl.DeviceIdType.MESH,
        )

    def put(self, j, products):
        for i, g in enumerate(products(part(1 - self.core, HALF))):
            self.sent[lax.rem(j, 2), i] = g.astype(BF)
        for i, g in enumerate(products(part(self.core, HALF))):
            self.kept[lax.rem(j, 3), i] = g

    def total(self, j, i, rows):
        return self.kept[lax.rem(j, 3), i, rows, :] + self.got[j, i, rows, :].astype(F32)


def exchange_steps(exchange, loads, early, compute, finish):
    j = pl.program_id(0)

    @pl.when(j == 0)
    def _():
        for load in loads:
            load.start()
        exchange.greet()
        for load in loads[:early]:
            load.wait()

    @pl.when(j >= 2)
    def _():
        exchange.copy(j - 2).wait()

    def late():
        @pl.when(j == 0)
        def _():
            for load in loads[early:]:
                load.wait()

    @pl.when(j < 2)
    def _():
        compute(j, late)

    @pl.when((j >= 2) & (j < NT))
    def _():
        finish(j - 2)
        compute(j, None)

    @pl.when(j < NT)
    def _():
        exchange.copy(j).start()

    @pl.when(j >= NT)
    def _():
        finish(j - 2)


def first_weights_kernel(
    at_any, byt_any, by_any, gate_ref, up_ref, wd_ref, home_ref, away_ref,
    at_ref, byt_ref, by_ref, act_ref, dg_ref, du_ref, load_sem, *exchange,
):
    exchange = Exchange(*exchange)
    pairs = ((by_any, by_ref), (at_any, at_ref), (byt_any, byt_ref))
    loads = [pltpu.make_async_copy(a, b, load_sem.at[n]) for n, (a, b) in enumerate(pairs)]

    def compute(j, late):
        for r in range(NC):
            rows = slice(r * CHUNK, (r + 1) * CHUNK)
            by_act = dot_nt(by_ref[rows, :], wd_ref[...])
            act_ref[rows, :], dg_ref[rows, :], du_ref[rows, :] = gated(gate_ref[rows, :], up_ref[rows, :], by_act)
        if late:
            late()
        exchange.put(
            j,
            lambda half: (dot(a[half, :], b[...]) for a, b in ((at_ref, dg_ref), (at_ref, du_ref), (byt_ref, act_ref))),
        )

    def finish(j):
        for i in range(3):
            home_ref[i] = exchange.total(j, i, part(exchange.chip, QUARTER))
            away_ref[i] = exchange.total(j, i, part(1 - exchange.chip, QUARTER)).astype(BF)

    exchange_steps(exchange, loads, 1, compute, finish)


def tile_now(j):
    return jnp.minimum(j, NT - 1)


def tile_done(j):
    return jnp.clip(j - 2, 0, NT - 1)


ANY = pl.BlockSpec(memory_space=pl.ANY)


def first_weights(at, byt, by, gate, up, wd, layer):
    tile = pl.BlockSpec((T, FT), lambda j: (0, tile_now(j)))
    out = pl.BlockSpec((3, QUARTER, FT), lambda j: (0, 0, tile_done(j)))
    return pl.pallas_call(
        first_weights_kernel,
        grid=(NT + 2,),
        in_specs=[ANY, ANY, ANY, tile, tile, pl.BlockSpec((None, FT, D), lambda j: (layer, tile_now(j), 0))],
        out_specs=[out, out],
        out_shape=[jax.ShapeDtypeStruct((3, QUARTER, FF), F32), jax.ShapeDtypeStruct((3, QUARTER, FF), BF)],
        scratch_shapes=[
            pltpu.VMEM((D, T), BF),
            pltpu.VMEM((D, T), BF),
            pltpu.VMEM((T, D), BF),
            *[pltpu.VMEM((T, FT), BF)] * 3,
            pltpu.SemaphoreType.DMA((3,)),
            *Exchange.scratch,
        ],
        compiler_params=params(collective_id=0),
        cost_estimate=cost(4, 80e6),
        name="first_weights",
    )(at, byt, by, gate, up, wd)


def last_weights_kernel(
    at_any, byt_any, a2_any, by2_any, at2_any, byt2_any, act_ref, dg_ref, du_ref, wg_ref, wu_ref, wd_ref, mine_ref, squares_ref,
    at_ref, byt_ref, a2_ref, by2_ref, at2_ref, byt2_ref, act2_ref, dg2_ref, du2_ref, load_sem, *exchange,
):
    exchange = Exchange(*exchange)
    pairs = (
        (a2_any, a2_ref), (by2_any, by2_ref), (at_any, at_ref), (at2_any, at2_ref), (byt_any, byt_ref), (byt2_any, byt2_ref),
    )
    loads = [pltpu.make_async_copy(a, b, load_sem.at[n]) for n, (a, b) in enumerate(pairs)]

    @pl.when(pl.program_id(0) == 0)
    def _():
        squares_ref[...] = jnp.zeros_like(squares_ref)

    def compute(j, late):
        for r in range(NC):
            rows = slice(r * CHUNK, (r + 1) * CHUNK)
            gate = dot(a2_ref[rows, :], wg_ref[...])
            up = dot(a2_ref[rows, :], wu_ref[...])
            by_act = dot_nt(by2_ref[rows, :], wd_ref[...])
            act2_ref[rows, :], dg2_ref[rows, :], du2_ref[rows, :] = gated(gate, up, by_act)
        if late:
            late()
        fours = ((at_ref, dg_ref, at2_ref, dg2_ref), (at_ref, du_ref, at2_ref, du2_ref), (byt_ref, act_ref, byt2_ref, act2_ref))
        exchange.put(j, lambda half: (dot(a[half, :], b[...]) + dot(c[half, :], d[...]) for a, b, c, d in fours))

    def finish(j):
        squares = squares_ref[...]
        for i in range(3):
            for r in range(4):
                rows = slice(r * HALF // 4, (r + 1) * HALF // 4)
                mine = exchange.total(j, i, rows).astype(BF)
                mine_ref[i, rows, :] = mine
                wide = mine.astype(F32)
                squares += jnp.sum((wide * wide).reshape(-1, 8, FT), 0)
        squares_ref[...] = squares

    exchange_steps(exchange, loads, 2, compute, finish)


def last_weights(at, byt, a2, by2, at2, byt2, act, dg, du, wg, wu, wd, layer):
    tile = pl.BlockSpec((T, FT), lambda j: (0, tile_now(j)))
    weight = pl.BlockSpec((None, D, FT), lambda j: (layer, 0, tile_now(j)))
    return pl.pallas_call(
        last_weights_kernel,
        grid=(NT + 2,),
        in_specs=[ANY] * 6
        + [tile, tile, tile, weight, weight, pl.BlockSpec((None, FT, D), lambda j: (layer, tile_now(j), 0))],
        out_specs=[pl.BlockSpec((3, HALF, FT), lambda j: (0, 0, tile_done(j))), pl.BlockSpec((8, FT), lambda j: (0, 0))],
        out_shape=[jax.ShapeDtypeStruct((3, HALF, FF), BF), jax.ShapeDtypeStruct((8, FT), F32)],
        scratch_shapes=[
            pltpu.VMEM((D, T), BF), pltpu.VMEM((D, T), BF), pltpu.VMEM((T, D), BF),
            pltpu.VMEM((T, D), BF), pltpu.VMEM((D, T), BF), pltpu.VMEM((D, T), BF),
            *[pltpu.VMEM((T, FT), BF)] * 3,
            pltpu.SemaphoreType.DMA((6,)),
            *Exchange.scratch,
        ],
        compiler_params=params(collective_id=1),
        cost_estimate=cost(9, 90e6),
        name="last_weights",
    )(at, byt, a2, by2, at2, byt2, act, dg, du, wg, wu, wd)


def adamw(w, m, v, g):
    m = 0.9 * m + 0.1 * g
    v = 0.95 * v + 0.05 * g * g
    step = m * lax.rsqrt(v + 1e-8) + 0.1 * w
    return (w - 0.02 * step).astype(BF), m, v


def adamw_kernel(ranges, n_alias, table_ref, factor_ref, *refs):
    n = len(ranges)
    gradients, refs = refs[:n], refs[n:]
    ins, outs, turned_ref = refs[:9], refs[9 + n_alias : 18 + n_alias], refs[-1]
    step = pl.program_id(0)
    for g_ref, (first, last) in zip(gradients, ranges, strict=True):

        @pl.when((step >= first) & (step < last))
        def _(g_ref=g_ref):
            factor = factor_ref[0]
            turned_ref[...] = g_ref[2].T
            for i in range(3):

                def some(r, _, i=i):
                    rows = pl.ds(pl.multiple_of(r * SOME, SOME), SOME)
                    g = (turned_ref[rows, :] if i == 2 else g_ref[i, rows, :]).astype(F32) * factor
                    new = adamw(ins[i][rows, :].astype(F32), ins[3 + i][rows, :], ins[6 + i][rows, :], g)
                    for which in range(3):
                        outs[3 * which + i][rows, :] = new[which]
                    return _

                lax.fori_loop(0, (BROAD if i == 2 else ROWS) // SOME, some, 0, unroll=UNROLL)


def adamw_steps(segments):
    steps = []
    for g, layer, row, start in segments:
        steps += [(layer, row + r, start + f) for r in range(g.shape[1] // ROWS) for f in range(g.shape[2] // BROAD)]
    return steps


def adamw_blocks(segments, table, begin, factor, arrays, so_far):
    ranges, steps = [], 0
    for g, *_ in segments:
        more = (g.shape[1] // ROWS) * (g.shape[2] // BROAD)
        ranges.append((steps, steps + more))
        steps += more

    def g_spec(g, start, stop):
        broad = g.shape[2] // BROAD

        def index(s, *_):
            own = jnp.clip(s - start, 0, stop - start - 1)
            return 0, own // broad, own % broad

        return pl.BlockSpec((3, ROWS, BROAD), index)

    wide = pl.BlockSpec((None, ROWS, BROAD), lambda s, t, _: (t[0, s + begin], t[1, s + begin], t[2, s + begin]))
    tall = pl.BlockSpec((None, BROAD, ROWS), lambda s, t, _: (t[0, s + begin], t[2, s + begin], t[1, s + begin]))
    nine = [wide, wide, tall] * 3
    gradients = [s[0] for s in segments]
    n = len(gradients)
    alias = {2 + n + 9 + i: i for i in range(9)} if so_far else {}
    shapes = [jax.ShapeDtypeStruct(a.shape, BF if i < 3 else F32) for i, a in enumerate(arrays)]
    return pl.pallas_call(
        functools.partial(adamw_kernel, ranges, len(so_far)),
        grid_spec=pltpu.PrefetchScalarGridSpec(
            num_scalar_prefetch=2,
            grid=(steps,),
            in_specs=[g_spec(g, *r) for g, r in zip(gradients, ranges, strict=True)] + nine + [pl.BlockSpec(memory_space=pl.ANY)] * len(so_far),
            out_specs=nine,
            scratch_shapes=[pltpu.VMEM((BROAD, ROWS), BF)],
        ),
        out_shape=shapes,
        input_output_aliases=alias,
        compiler_params=params(),
        cost_estimate=cost(2.5 * steps / (4 * 4), 190e6 * steps / (4 * 4)),
        name="adamw",
    )(table, factor, *gradients, *arrays, *so_far)


def solution(mesh):
    def step(x, dy, *arrays):
        wg, wu, wd = arrays[:3]
        me = lax.axis_index("dp")
        chip, core = me >> 1, me & 1

        def swap_x(a):
            return lax.ppermute(a, "dp", X_SWAP)

        def swap_core(a):
            return lax.ppermute(a, "dp", CORE_SWAP)

        h0, by2 = x[0], dy[0]
        by2_other = swap_x(by2)
        act0, gate0, up0, a0t = gate_up(h0, wg, wu, 0)
        h1, a1, a1t = down(act0, wd, h0, 0)
        h1_other = swap_x(h1)
        act1, dg1, du1, by2t = hidden(a1, by2, wg, wu, wd, 1)
        by1, by1t = states(dg1, du1, wg, wu, h1, by2, 1)
        home, away = first_weights(a0t, by1t, by1, gate0, up0, wd, 0)
        far = swap_x(away)
        a1o, a1ot, by2ot = norm_turn(h1_other, by2_other)
        half, squares1 = last_weights(a1t, by2t, a1o, by2_other, a1ot, by2ot, act1, dg1, du1, wg, wu, wd, 1)
        core_half = swap_core(half)
        quarter = (home + far.astype(F32)).astype(BF)
        squares0 = jnp.sum(jnp.square(quarter.astype(F32)))

        squares0 = squares0.reshape(1, 1)
        squares0 = squares0 + swap_x(squares0)
        squares = squares0 + jnp.sum(squares1).reshape(1, 1)
        squares = (squares + swap_core(squares)).reshape(1)
        count = sum(a.size for a in arrays[:3])
        factor = jnp.minimum(1.0, 0.5 * lax.rsqrt(squares / count + 1e-30))

        far_quarter = swap_x(quarter)
        core_quarter = swap_core(quarter)
        core_far = swap_core(far_quarter)

        groups = [
            [(half, 1, 0, 0), (quarter, 0, 0, 0), (core_half, 1, 2, 0), (core_quarter, 0, 2, 0)],
            [(far_quarter, 0, 1, 0), (core_far, 0, 3, 0)],
        ]
        steps = [adamw_steps(group) for group in groups]
        table = np.array(sum(steps, []), np.int32).T
        owns = jnp.where(table[0] == 0, 2 * core + chip, 2 * core).astype(jnp.int32)
        table = jnp.asarray(table) ^ (jnp.asarray([[0], [1], [0]], jnp.int32) * owns)
        out, begin = [], 0
        for n, group in enumerate(groups):
            out = adamw_blocks(group, table, begin, factor, arrays, out)
            begin += len(steps[n])
        return tuple(out)

    return jax.shard_map(
        step,
        mesh=mesh,
        in_specs=(P(("rep", "dp"), None, None),) * 2 + (P(None, None, None),) * 9,
        out_specs=(P("rep", None, None),) * 9,
        check_vma=False,
    )
```

time: 790 us -> 601 us (0.76)
  waiting for transfers between devices: 176 us -> 99.5 us
  Pallas kernels: 513 us -> 472 us
  starting transfers between devices: 46.8 us -> 7.17 us
  other arithmetic: 37 us -> 10.8 us
    ppermute x7 -> x5, waiting for transfers between devices: 176 us -> 99.1 us  [swap_x(): return lax.ppermute(a, 'dp', X_SWAP)]
    ppermute x7 -> x5, starting transfers between devices: 42.5 us -> 5.7 us  [swap_x(): return lax.ppermute(a, 'dp', X_SWAP)]
    pallas_call x6 -> x2, Pallas kernels: 218 us -> 197 us  [the longest x1 128 us: last_weights(): pl.pallas_call(last_weights_kernel, grid=(NT + 2,), in_specs=[ANY] * 6 +...]
    pallas_call x4 -> x2, Pallas kernels: 150 us -> 130 us  [adamw_blocks(): pl.pallas_call(functools.partial(adamw_kernel, ranges, len(so_far)), grid...]
    reduce_sum x5 -> x2, other arithmetic: 28.1 us -> 10.2 us  [the longest x1 9.55 us: step(): squares0 = jnp.sum(jnp.square(quarter.astype(F32)))]
    convert_element_type x2 -> x0, other arithmetic: 8.28 us -> none  [step(): away = (piece(keep, away) + piece(got, away)).astype(BF)]
  transfers between devices with their start and end apart: 20 -> 9, of which waited for: 6 -> 3; matrix products, arithmetic and copies ran while one was open for 5% -> 2% of each run, Pallas kernels for 40% -> 74%
where the time goes in v2:
time: 601 us; the launch traced here: 594 us
  Pallas kernels  472 us (79%)
  waiting for transfers between devices  99.5 us (17%)
  other arithmetic  10.8 us (2%)
  starting transfers between devices  7.17 us (1%)
    pallas_call x2, Pallas kernels, adamw_blocks(): pl.pallas_call(functools.partial(adamw_kernel, ranges, len(so_far)), grid...  130 us
    pallas_call x1, Pallas kernels, last_weights(): pl.pallas_call(last_weights_kernel, grid=(NT + 2,), in_specs=[ANY] * 6 +...  128 us
    ppermute x5, waiting for transfers between devices, swap_x(): return lax.ppermute(a, 'dp', X_SWAP)  99.1 us
    pallas_call x1, Pallas kernels, first_weights(): pl.pallas_call(first_weights_kernel, grid=(NT + 2,), in_specs=[ANY, ANY,...  69.4 us
    pallas_call x1, Pallas kernels, hidden(): pl.pallas_call(hidden_kernel, grid=(NT,), in_specs=[whole((T, D)), whole(...  46.3 us
    pallas_call x1, Pallas kernels, states(): pl.pallas_call(states_kernel, grid=(T // tm,), in_specs=[hidden_rows, hid...  35.1 us
    pallas_call x1, Pallas kernels, gate_up(): pl.pallas_call(gate_up_kernel, grid=(NT,), in_specs=[whole((T, D)), weigh...  34.2 us
    pallas_call x1, Pallas kernels, down(): pl.pallas_call(down_kernel, grid=(NC,), in_specs=[pl.BlockSpec((CHUNK, FF...  20.4 us
  transfers between devices with their start and end apart: 9, of which 3 were waited for; matrix products, arithmetic and copies ran while one was open for 2% of the time, Pallas kernels for 74%

profile of v2, /device:TPU:0, one launch (start us, length us, event | category | flops | bytes accessed | tf_op | source)
XLA Modules:
  0.0 593.6 jit_solution(15133359113198887794)
XLA Ops:
  0.6 3.3 collective-permute-start.3
  4.0 34.2 %gate_up.1 = (bf16[2048,2816]{1,0:T(8,128)(2,1)}, f32[2048,2816]{1,0:T(8,128)}, f32[2048,2816]{1,0:T(8,128)}, bf16[1024,2048]{1,0:T(8,128)(2,1)}) custom-call(bf16[2048,1024]{1,0:T(8,128)(2,1)} %bitcast.5, bf16[2,1024,2816]{2,1,0:T(8,128)(2,1)} %refs_2_.1, bf16[2,1024,2816]{2,1,0:T(8,128)(2,1)} %refs_3_.1), custom_call_target="tpu_custom_call" | custom-call | flops 23622320128 | bytes 75000000 | tf_op jit(solution)/shard_map/gate_up/pallas_call | solution.py:74
  38.1 20.4 %down.1 = (bf16[2048,1024]{1,0:T(8,128)(2,1)}, bf16[2048,1024]{1,0:T(8,128)(2,1)}, bf16[1024,2048]{1,0:T(8,128)(2,1)}) custom-call(bf16[2048,2816]{1,0:T(8,128)(2,1)} %get-tuple-element.39.act_ref, bf16[2,2816,1024]{2,1,0:T(8,128)(2,1)} %refs_4_.3, bf16[2048,1024]{1,0:T(8,128)(2,1)} %bitcast.6), custom_call_target="tpu_custom_call" | custom-call | flops 11811160064 | bytes 30000000 | tf_op jit(solution)/shard_map/down/pallas_call | solution.py:102
  58.6 0.0 collective-permute-start.2
  58.6 46.3 %hidden.1 = (bf16[2048,2816]{1,0:T(8,128)(2,1)}, bf16[2048,2816]{1,0:T(8,128)(2,1)}, bf16[2048,2816]{1,0:T(8,128)(2,1)}, bf16[1024,2048]{1,0:T(8,128)(2,1)}) custom-call(bf16[2048,1024]{1,0:T(8,128)(2,1)} %get-tuple-element.40.a_ref, bf16[2048,1024]{1,0:T(8,128)(2,1)} %bitcast.8, bf16[2,1024,2816]{2,1,0:T(8,128)(2,1)} %refs_2_.1, ...), custom_call_target="tpu_custom_call" | custom-call | flops 35433480192 | bytes 60000000 | tf_op jit(solution)/shard_map/hidden/pallas_call | solution.py:166
  104.9 35.1 %states.1 = (bf16[2048,1024]{1,0:T(8,128)(2,1)}, bf16[1024,2048]{1,0:T(8,128)(2,1)}) custom-call(bf16[2048,2816]{1,0:T(8,128)(2,1)} %get-tuple-element.41.dg_ref, bf16[2048,2816]{1,0:T(8,128)(2,1)} %get-tuple-element.42.du_ref, bf16[2,1024,2816]{2,1,0:T(8,128)(2,1)} %refs_2_.1, bf16[2,1024,2816]{2,1,0:T(8,128)(2,1)} %refs_3_.1, ...), custom_call_target="tpu_custom_call" | custom-call | flops 23622320128 | bytes 45000000 | tf_op jit(solution)/shard_map/states/pallas_call | solution.py:195
  140.0 69.4 %first_weights.1 = (f32[3,256,2816]{2,1,0:T(8,128)}, bf16[3,256,2816]{2,1,0:T(8,128)(2,1)}) custom-call(bf16[1024,2048]{1,0:T(8,128)(2,1)} %get-tuple-element.38.at_any, bf16[1024,2048]{1,0:T(8,128)(2,1)} %get-tuple-element.44.byt_any, bf16[2048,1024]{1,0:T(8,128)(2,1)} %get-tuple-element.45.by_any, f32[2048,2816]{1,0:T(8,128)} %get-tuple-element.46.gate_ref, ...), custom_call_target="tpu_custom_call" | custom-call | flops 47244640256 | bytes 80000000 | tf_op jit(solution)/shard_map/first_weights/pallas_call | solution.py:336
  209.4 2.0 collective-permute-start
  211.4 0.0 collective-permute-done.3.x_ref.by2_any
  211.4 0.0 collective-permute-done.2.h_ref
  211.4 8.9 %norm_turn.1 = (bf16[2048,1024]{1,0:T(8,128)(2,1)}, bf16[1024,2048]{1,0:T(8,128)(2,1)}, bf16[1024,2048]{1,0:T(8,128)(2,1)}) custom-call(bf16[2048,1024]{1,0:T(8,128)(2,1)} %collective-permute-done.2.h_ref, bf16[2048,1024]{1,0:T(8,128)(2,1)} %collective-permute-done.3.x_ref.by2_any), custom_call_target="tpu_custom_call" | custom-call | flops 4724464128 | bytes 20000000 | tf_op jit(solution)/shard_map/norm_turn/pallas_call | solution.py:132
  220.4 127.7 %last_weights.1 = (bf16[3,512,2816]{2,1,0:T(8,128)(2,1)}, f32[8,256]{1,0:T(8,128)}) custom-call(bf16[1024,2048]{1,0:T(8,128)(2,1)} %get-tuple-element.50.at_any, bf16[1024,2048]{1,0:T(8,128)(2,1)} %get-tuple-element.51.byt_any, bf16[2048,1024]{1,0:T(8,128)(2,1)} %get-tuple-element.52.a2_any, bf16[2048,1024]{1,0:T(8,128)(2,1)} %collective-permute-done.3.x_ref.by2_any, ...), custom_call_target="tpu_custom_call" | custom-call | flops 106300440576 | bytes 90000000 | tf_op jit(solution)/shard_map/last_weights/pallas_call | solution.py:399
  348.1 0.0 copy-start.3
  348.1 0.0 copy-start.1
  348.1 0.0 copy-start.2
  348.1 0.0 copy-start
  348.1 0.4 collective-permute-start.7
  348.5 0.0 collective-permute-done
  348.5 9.6 %multiply_reduce_fusion = (f32[]{:T(128)}, bf16[3,256,2816]{2,1,0:T(8,128)(2,1)}) fusion(f32[3,256,2816]{2,1,0:T(8,128)} %get-tuple-element.48, bf16[3,256,2816]{2,1,0:T(8,128)(2,1)} %collective-permute-done), kind=kLoop, calls=%fused_computation | loop fusion | flops 12976127 | bytes 17301508 | tf_op jit(solution)/shard_map/reduce_sum | solution.py:522
  358.1 0.0 collective-permute-start.5
  358.1 0.1 collective-permute-start.8
  358.2 95.6 %collective-permute-done.5.refs_0_ = bf16[3,256,2816]{2,1,0:T(8,128)(2,1)} collective-permute-done((bf16[3,256,2816]{2,1,0:T(8,128)(2,1)}, bf16[3,256,2816]{2,1,0:T(8,128)(2,1)}, u32[]{:S(2)}, u32[]{:S(2)}) %collective-permute-start.5) | collective-permute-done | bytes 4325408 | tf_op jit(solution)/shard_map/ppermute | solution.py:504
  453.8 0.0 collective-permute-start.6
  453.8 0.0 copy-done.3
  453.8 0.0 copy-done.1
  453.8 0.0 copy-done.2
  453.8 0.7 multiply_xor_fusion.table_ref
  454.5 0.0 copy-done
  454.5 0.6 reduce_sum.19
  455.1 0.3 collective-permute-start.1
  455.4 3.5 collective-permute-done.1
  460.8 1.0 collective-permute-start.4
  461.8 0.3 collective-permute-done.4
  462.8 0.0 collective-permute-done.8.refs_3_
  462.8 0.0 collective-permute-done.7.refs_2_
  462.8 97.1 %adamw.2 = (bf16[2,1024,2816]{2,1,0:T(8,128)(2,1)}, bf16[2,1024,2816]{2,1,0:T(8,128)(2,1)}, bf16[2,2816,1024]{2,1,0:T(8,128)(2,1)}, f32[2,1024,2816]{2,1,0:T(8,1...) custom-call(s32[3,16]{1,0:T(4,128)} %multiply_xor_fusion.table_ref, ...), custom_call_target="tpu_custom_call" | custom-call | flops 22145925120 | bytes 142500000 | tf_op jit(solution)/shard_map/adamw/pallas_call | solution.py:480
  559.9 0.0 collective-permute-done.6.refs_1_
  559.9 33.2 %adamw.3 = (bf16[2,1024,2816]{2,1,0:T(8,128)(2,1)}, bf16[2,1024,2816]{2,1,0:T(8,128)(2,1)}, bf16[2,2816,1024]{2,1,0:T(8,128)(2,1)}, f32[2,1024,2816]{2,1,0:T(8,1...) custom-call(s32[3,16]{1,0:T(4,128)} %multiply_xor_fusion.table_ref, ...), custom_call_target="tpu_custom_call", output_to_operand_aliasing={{0}: (13, {}), {1}: (14, {}), {2}: (15, {}), {3}: (16, {}),... | custom-call | flops 7381975040 | bytes 47500000 | tf_op jit(solution)/shard_map/adamw/pallas_call | solution.py:480
  (1 shorter events, 0.0 us)
Async XLA Ops:
  0.6 210.8 %collective-permute-start.3 = (bf16[2048,1024]{1,0:T(8,128)(2,1)}, bf16[2048,1024]{1,0:T(8,128)(2,1)}, u32[]{:S(2)}, u32[]{:S(2)}) collective-permute-start(bf16[2048,1024]{1,0:T(8,128)(2,1)} %bitcast.7), channel_id=1, source_target_pairs={{0,2},{2,0},{1,3},{3,1},{4,6},{6,4},{5,7},{7,5}} | collective-permute-start | bytes 12582920 | tf_op jit(solution)/shard_map/ppermute | solution.py:504
  58.6 152.9 %collective-permute-start.2 = (bf16[2048,1024]{1,0:T(8,128)(2,1)}, bf16[2048,1024]{1,0:T(8,128)(2,1)}, u32[]{:S(2)}, u32[]{:S(2)}) collective-permute-start(bf16[2048,1024]{1,0:T(8,128)(2,1)} %get-tuple-element.43.h_ref), channel_id=1, source_target_pairs={{0,2},{2,0},{1,3},{3,1},{4,6},{6,4},{5,7},{7,5}} | collective-permute-start | bytes 12582920 | tf_op jit(solution)/shard_map/ppermute | solution.py:504
  209.4 139.1 %collective-permute-start = (bf16[3,256,2816]{2,1,0:T(8,128)(2,1)}, bf16[3,256,2816]{2,1,0:T(8,128)(2,1)}, u32[]{:S(2)}, u32[]{:S(2)}) collective-permute-start(bf16[3,256,2816]{2,1,0:T(8,128)(2,1)} %get-tuple-element.49), channel_id=1, source_target_pairs={{0,2},{2,0},{1,3},{3,1},{4,6},{6,4},{5,7},{7,5}} | collective-permute-start | bytes 12976136 | tf_op jit(solution)/shard_map/ppermute | solution.py:504
  348.1 105.7 %copy-start.3 = (pred[16]{0:T(512)(128)(4,1)S(1)}, pred[16]{0:T(512)(128)(4,1)}, u32[]{:S(2)}) copy-start(pred[16]{0:T(512)(128)(4,1)} %constant.28.clone) | copy-start | bytes 52
  348.1 105.7 %copy-start.1 = (s32[3,16]{1,0:T(4,128)S(1)}, s32[3,16]{1,0:T(4,128)}, u32[]{:S(2)}) copy-start(s32[3,16]{1,0:T(4,128)} %constant.29.clone) | copy-start | bytes 580
  348.1 105.7 %copy-start.2 = (s32[3]{0:T(128)S(1)}, s32[3]{0:T(128)}, u32[]{:S(2)}) copy-start(s32[3]{0:T(128)} %constant.33) | copy-start | bytes 40
  348.1 106.4 %copy-start = (f32[8,256]{1,0:T(8,128)S(1)}, f32[8,256]{1,0:T(8,128)}, u32[]{:S(2)}) copy-start(f32[8,256]{1,0:T(8,128)} %get-tuple-element.56) | copy-start | bytes 24580
  348.1 114.7 %collective-permute-start.7 = (bf16[3,512,2816]{2,1,0:T(8,128)(2,1)}, bf16[3,512,2816]{2,1,0:T(8,128)(2,1)}, u32[]{:S(2)}, u32[]{:S(2)}) collective-permute-start(bf16[3,512,2816]{2,1,0:T(8,128)(2,1)} %get-tuple-element.57.refs_0_), channel_id=1, source_target_pairs={{0,1},{1,0},{2,3},{3,2},{4,5},{5,4},{6,7},{7,6}} | collective-permute-start | bytes 25952264 | tf_op jit(solution)/shard_map/ppermute | solution.py:507
  358.1 95.7 %collective-permute-start.5 = (bf16[3,256,2816]{2,1,0:T(8,128)(2,1)}, bf16[3,256,2816]{2,1,0:T(8,128)(2,1)}, u32[]{:S(2)}, u32[]{:S(2)}) collective-permute-start(bf16[3,256,2816]{2,1,0:T(8,128)(2,1)} %get-tuple-element.68.refs_1_), channel_id=1, source_target_pairs={{0,2},{2,0},{1,3},{3,1},{4,6},{6,4},{5,7},{7,5}} | collective-permute-start | bytes 12976136 | tf_op jit(solution)/shard_map/ppermute | solution.py:504
  358.1 104.7 %collective-permute-start.8 = (bf16[3,256,2816]{2,1,0:T(8,128)(2,1)}, bf16[3,256,2816]{2,1,0:T(8,128)(2,1)}, u32[]{:S(2)}, u32[]{:S(2)}) collective-permute-start(bf16[3,256,2816]{2,1,0:T(8,128)(2,1)} %get-tuple-element.68.refs_1_), channel_id=1, source_target_pairs={{0,1},{1,0},{2,3},{3,2},{4,5},{5,4},{6,7},{7,6}} | collective-permute-start | bytes 12976136 | tf_op jit(solution)/shard_map/ppermute | solution.py:507
  453.8 106.1 %collective-permute-start.6 = (bf16[3,256,2816]{2,1,0:T(8,128)(2,1)}, bf16[3,256,2816]{2,1,0:T(8,128)(2,1)}, u32[]{:S(2)}, u32[]{:S(2)}) collective-permute-start(bf16[3,256,2816]{2,1,0:T(8,128)(2,1)} %collective-permute-done.5.refs_0_), channel_id=1, source_target_pairs={{0,1},{1,0},{2,3},{3,2},{4,5},{5,4},{6,7},{7,6}} | collective-permute-start | bytes 12976136 | tf_op jit(solution)/shard_map/ppermute | solution.py:507
  455.1 3.8 collective-permute-start.1
  460.8 1.3 collective-permute-start.4

commit v3 on v2

--- a/solution.py
+++ b/solution.py
@@ -46,99 +46,81 @@
     return wide * lax.rsqrt(jnp.mean(wide * wide, -1, keepdims=True) + EPS)
 
 
+def part(index, size):
+    return pl.ds(pl.multiple_of(index * size, size), size)
+
+
+def tile_now(j):
+    return jnp.minimum(j, NT - 1)
+
+
 def whole(shape):
     return pl.BlockSpec(shape, lambda *_: (0,) * len(shape))
 
 
-def gate_up_kernel(h_ref, wg_ref, wu_ref, act_ref, gate_ref, up_ref, at_ref, a_ref):
-    @pl.when(pl.program_id(0) == 0)
-    def _():
-        for r in range(NC):
-            rows = slice(r * CHUNK, (r + 1) * CHUNK)
+def forward_kernel(
+    h_ref, wg_ref, wu_ref, wd_ref, act_ref, silu_ref, slope_ref, at_ref, out_ref, a1_ref, a1t_ref, a_ref, total_ref
+):
+    j = pl.program_id(0)
+
+    @pl.when(j == 0)
+    def _():
+        def some(r, _):
+            rows = part(r, TURN)
             a = norm(h_ref[rows, :]).astype(BF)
             a_ref[rows, :] = a
             at_ref[:, rows] = a.T
-
-    for r in range(NC):
-        rows = slice(r * CHUNK, (r + 1) * CHUNK)
-        gate = dot(a_ref[rows, :], wg_ref[...])
-        up = dot(a_ref[rows, :], wu_ref[...])
-        gate_ref[rows, :] = gate
-        up_ref[rows, :] = up
-        act_ref[rows, :] = (gate * jax.nn.sigmoid(gate) * up).astype(BF)
-
-
-def gate_up(h, wg, wu, layer):
-    weight = pl.BlockSpec((None, D, FT), lambda j: (layer, 0, j))
-    tile = pl.BlockSpec((T, FT), lambda j: (0, j))
-    return pl.pallas_call(
-        gate_up_kernel,
-        grid=(NT,),
-        in_specs=[whole((T, D)), weight, weight],
-        out_specs=[tile, tile, tile, whole((D, T))],
+            total_ref[rows, :] = jnp.zeros((TURN, D), F32)
+            return _
+
+        lax.fori_loop(0, T // TURN, some, 0)
+
+    @pl.when(j < NT)
+    def _():
+        for r in range(NC):
+            rows = slice(r * CHUNK, (r + 1) * CHUNK)
+            gate = dot(a_ref[rows, :], wg_ref[...])
+            up = dot(a_ref[rows, :], wu_ref[...])
+            sig = jax.nn.sigmoid(gate)
+            silu = gate * sig
+            act_ref[rows, :] = (silu * up).astype(BF)
+            silu_ref[rows, :] = silu
+            slope_ref[rows, :] = up * (sig + silu * (1.0 - sig))
+            total_ref[rows, :] += dot(act_ref[rows, :], wd_ref[...])
+
+    @pl.when(j >= NT)
+    def _():
+        rows = part(j - NT, CHUNK)
+        h = h_ref[rows, :] + total_ref[rows, :].astype(BF)
+        out_ref[...] = h
+        a = norm(h).astype(BF)
+        a1_ref[...] = a
+        a1t_ref[...] = a.T
+
+
+def forward(h, wg, wu, wd, layer):
+    weight = pl.BlockSpec((None, D, FT), lambda j: (layer, 0, tile_now(j)))
+    tile = pl.BlockSpec((None, T, FT), lambda j: (tile_now(j), 0, 0))
+    rows = pl.BlockSpec((CHUNK, D), lambda j: (jnp.maximum(j - NT, 0), 0))
+    return pl.pallas_call(
+        forward_kernel,
+        grid=(NT + NC,),
+        in_specs=[whole((T, D)), weight, weight, pl.BlockSpec((None, FT, D), lambda j: (layer, tile_now(j), 0))],
+        out_specs=[tile, tile, tile, whole((D, T)), rows, rows, pl.BlockSpec((D, CHUNK), lambda j: (0, jnp.maximum(j - NT, 0)))],
         out_shape=[
-            jax.ShapeDtypeStruct((T, FF), BF),
-            jax.ShapeDtypeStruct((T, FF), F32),
-            jax.ShapeDtypeStruct((T, FF), F32),
+            jax.ShapeDtypeStruct((NT, T, FT), BF),
+            jax.ShapeDtypeStruct((NT, T, FT), F32),
+            jax.ShapeDtypeStruct((NT, T, FT), F32),
             jax.ShapeDtypeStruct((D, T), BF),
-        ],
-        scratch_shapes=[pltpu.VMEM((T, D), BF)],
-        compiler_params=params(),
-        cost_estimate=cost(2, 75e6),
-        name="gate_up",
-    )(h, wg, wu)
-
-
-def down_kernel(act_ref, w_ref, h_ref, out_ref, a_ref, at_ref):
-    h = h_ref[...] + dot(act_ref[...], w_ref[...]).astype(BF)
-    out_ref[...] = h
-    a = norm(h).astype(BF)
-    a_ref[...] = a
-    at_ref[...] = a.T
-
-
-def down(act, w, h, layer):
-    rows = pl.BlockSpec((CHUNK, D), lambda i: (i, 0))
-    return pl.pallas_call(
-        down_kernel,
-        grid=(NC,),
-        in_specs=[
-            pl.BlockSpec((CHUNK, FF), lambda i: (i, 0)),
-            pl.BlockSpec((None, FF, D), lambda i: (layer, 0, 0)),
-            rows,
-        ],
-        out_specs=[rows, rows, pl.BlockSpec((D, CHUNK), lambda i: (0, i))],
-        out_shape=[
             jax.ShapeDtypeStruct((T, D), BF),
             jax.ShapeDtypeStruct((T, D), BF),
             jax.ShapeDtypeStruct((D, T), BF),
         ],
+        scratch_shapes=[pltpu.VMEM((T, D), BF), pltpu.VMEM((T, D), F32)],
         compiler_params=params(),
-        cost_estimate=cost(1, 30e6),
-        name="down",
-    )(act, w, h)
-
-
-def norm_turn_kernel(h_ref, x_ref, a_ref, at_ref, xt_ref):
-    a = norm(h_ref[...]).astype(BF)
-    a_ref[...] = a
-    at_ref[...] = a.T
-    xt_ref[...] = x_ref[...].T
-
-
-def norm_turn(h, x):
-    rows = pl.BlockSpec((CHUNK, D), lambda i: (i, 0))
-    columns = pl.BlockSpec((D, CHUNK), lambda i: (0, i))
-    return pl.pallas_call(
-        norm_turn_kernel,
-        grid=(NC,),
-        in_specs=[rows, rows],
-        out_specs=[rows, columns, columns],
-        out_shape=[jax.ShapeDtypeStruct((T, D), BF), jax.ShapeDtypeStruct((D, T), BF), jax.ShapeDtypeStruct((D, T), BF)],
-        compiler_params=params(),
-        cost_estimate=cost(0.4, 20e6),
-        name="norm_turn",
-    )(h, x)
+        cost_estimate=cost(3, 90e6),
+        name="forward",
+    )(h, wg, wu, wd)
 
 
 def gated(gate, up, by_act):
@@ -209,8 +191,7 @@
     return lax.div(me, 2), lax.rem(me, 2), me + 1 - 2 * lax.rem(me, 2)
 
 
-def part(index, size):
-    return pl.ds(pl.multiple_of(index * size, size), size)
+ORDER_OF_THREE = (2, 0, 1)
 
 
 class Exchange:
@@ -243,16 +224,16 @@
         )
 
     def put(self, j, products):
-        for i, g in enumerate(products(part(1 - self.core, HALF))):
+        for i, g in zip(ORDER_OF_THREE, products(part(1 - self.core, HALF))):
             self.sent[lax.rem(j, 2), i] = g.astype(BF)
-        for i, g in enumerate(products(part(self.core, HALF))):
+        for i, g in zip(ORDER_OF_THREE, products(part(self.core, HALF))):
             self.kept[lax.rem(j, 3), i] = g
 
     def total(self, j, i, rows):
         return self.kept[lax.rem(j, 3), i, rows, :] + self.got[j, i, rows, :].astype(F32)
 
 
-def exchange_steps(exchange, loads, early, compute, finish):
+def exchange_steps(exchange, loads, early, prepare, compute, finish):
     j = pl.program_id(0)
 
     @pl.when(j == 0)
@@ -262,53 +243,39 @@
         exchange.greet()
         for load in loads[:early]:
             load.wait()
+        if prepare:
+            prepare()
+        for load in loads[early:]:
+            load.wait()
 
     @pl.when(j >= 2)
     def _():
         exchange.copy(j - 2).wait()
-
-    def late():
-        @pl.when(j == 0)
-        def _():
-            for load in loads[early:]:
-                load.wait()
-
-    @pl.when(j < 2)
-    def _():
-        compute(j, late)
-
-    @pl.when((j >= 2) & (j < NT))
-    def _():
         finish(j - 2)
-        compute(j, None)
 
     @pl.when(j < NT)
     def _():
+        compute(j)
         exchange.copy(j).start()
 
-    @pl.when(j >= NT)
-    def _():
-        finish(j - 2)
-
 
 def first_weights_kernel(
-    at_any, byt_any, by_any, gate_ref, up_ref, wd_ref, home_ref, away_ref,
-    at_ref, byt_ref, by_ref, act_ref, dg_ref, du_ref, load_sem, *exchange,
+    at_any, byt_any, by_any, act_ref, silu_ref, slope_ref, wd_ref, home_ref, away_ref, at_ref, byt_ref, by_ref, dg_ref, du_ref,
+    load_sem, *exchange,
 ):
     exchange = Exchange(*exchange)
     pairs = ((by_any, by_ref), (at_any, at_ref), (byt_any, byt_ref))
     loads = [pltpu.make_async_copy(a, b, load_sem.at[n]) for n, (a, b) in enumerate(pairs)]
 
-    def compute(j, late):
+    def compute(j):
         for r in range(NC):
             rows = slice(r * CHUNK, (r + 1) * CHUNK)
-            by_act = dot_nt(by_ref[rows, :], wd_ref[...])
-            act_ref[rows, :], dg_ref[rows, :], du_ref[rows, :] = gated(gate_ref[rows, :], up_ref[rows, :], by_act)
-        if late:
-            late()
+            by_act = dot_nt(by_ref[rows, :], wd_ref[...]).astype(BF).astype(F32)
+            dg_ref[rows, :] = (by_act * slope_ref[rows, :]).astype(BF)
+            du_ref[rows, :] = (by_act * silu_ref[rows, :]).astype(BF)
         exchange.put(
             j,
-            lambda half: (dot(a[half, :], b[...]) for a, b in ((at_ref, dg_ref), (at_ref, du_ref), (byt_ref, act_ref))),
+            lambda half: (dot(a[half, :], b[...]) for a, b in ((byt_ref, act_ref), (at_ref, dg_ref), (at_ref, du_ref))),
         )
 
     def finish(j):
@@ -316,11 +283,7 @@
             home_ref[i] = exchange.total(j, i, part(exchange.chip, QUARTER))
             away_ref[i] = exchange.total(j, i, part(1 - exchange.chip, QUARTER)).astype(BF)
 
-    exchange_steps(exchange, loads, 1, compute, finish)
-
-
-def tile_now(j):
-    return jnp.minimum(j, NT - 1)
+    exchange_steps(exchange, loads, 1, None, compute, finish)
 
 
 def tile_done(j):
@@ -330,53 +293,58 @@
 ANY = pl.BlockSpec(memory_space=pl.ANY)
 
 
-def first_weights(at, byt, by, gate, up, wd, layer):
-    tile = pl.BlockSpec((T, FT), lambda j: (0, tile_now(j)))
+def first_weights(at, byt, by, act, silu, slope, wd, layer):
+    tile = pl.BlockSpec((None, T, FT), lambda j: (tile_now(j), 0, 0))
     out = pl.BlockSpec((3, QUARTER, FT), lambda j: (0, 0, tile_done(j)))
     return pl.pallas_call(
         first_weights_kernel,
         grid=(NT + 2,),
-        in_specs=[ANY, ANY, ANY, tile, tile, pl.BlockSpec((None, FT, D), lambda j: (layer, tile_now(j), 0))],
+        in_specs=[ANY, ANY, ANY, tile, tile, tile, pl.BlockSpec((None, FT, D), lambda j: (layer, tile_now(j), 0))],
         out_specs=[out, out],
         out_shape=[jax.ShapeDtypeStruct((3, QUARTER, FF), F32), jax.ShapeDtypeStruct((3, QUARTER, FF), BF)],
         scratch_shapes=[
             pltpu.VMEM((D, T), BF),
             pltpu.VMEM((D, T), BF),
             pltpu.VMEM((T, D), BF),
-            *[pltpu.VMEM((T, FT), BF)] * 3,
+            *[pltpu.VMEM((T, FT), BF)] * 2,
             pltpu.SemaphoreType.DMA((3,)),
             *Exchange.scratch,
         ],
         compiler_params=params(collective_id=0),
         cost_estimate=cost(4, 80e6),
         name="first_weights",
-    )(at, byt, by, gate, up, wd)
+    )(at, byt, by, act, silu, slope, wd)
 
 
 def last_weights_kernel(
-    at_any, byt_any, a2_any, by2_any, at2_any, byt2_any, act_ref, dg_ref, du_ref, wg_ref, wu_ref, wd_ref, mine_ref, squares_ref,
+    at_any, byt_any, h2_any, by2_any, act_ref, dg_ref, du_ref, wg_ref, wu_ref, wd_ref, mine_ref, squares_ref,
     at_ref, byt_ref, a2_ref, by2_ref, at2_ref, byt2_ref, act2_ref, dg2_ref, du2_ref, load_sem, *exchange,
 ):
     exchange = Exchange(*exchange)
-    pairs = (
-        (a2_any, a2_ref), (by2_any, by2_ref), (at_any, at_ref), (at2_any, at2_ref), (byt_any, byt_ref), (byt2_any, byt2_ref),
-    )
+    pairs = ((h2_any, a2_ref), (by2_any, by2_ref), (at_any, at_ref), (byt_any, byt_ref))
     loads = [pltpu.make_async_copy(a, b, load_sem.at[n]) for n, (a, b) in enumerate(pairs)]
 
-    @pl.when(pl.program_id(0) == 0)
-    def _():
+    def prepare():
         squares_ref[...] = jnp.zeros_like(squares_ref)
 
-    def compute(j, late):
+        def some(r, _):
+            rows = part(r, TURN)
+            byt2_ref[:, rows] = by2_ref[rows, :].T
+            a = norm(a2_ref[rows, :]).astype(BF)
+            a2_ref[rows, :] = a
+            at2_ref[:, rows] = a.T
+            return _
+
+        lax.fori_loop(0, T // TURN, some, 0)
+
+    def compute(j):
         for r in range(NC):
             rows = slice(r * CHUNK, (r + 1) * CHUNK)
             gate = dot(a2_ref[rows, :], wg_ref[...])
             up = dot(a2_ref[rows, :], wu_ref[...])
             by_act = dot_nt(by2_ref[rows, :], wd_ref[...])
             act2_ref[rows, :], dg2_ref[rows, :], du2_ref[rows, :] = gated(gate, up, by_act)
-        if late:
-            late()
-        fours = ((at_ref, dg_ref, at2_ref, dg2_ref), (at_ref, du_ref, at2_ref, du2_ref), (byt_ref, act_ref, byt2_ref, act2_ref))
+        fours = ((byt_ref, act_ref, byt2_ref, act2_ref), (at_ref, dg_ref, at2_ref, dg2_ref), (at_ref, du_ref, at2_ref, du2_ref))
         exchange.put(j, lambda half: (dot(a[half, :], b[...]) + dot(c[half, :], d[...]) for a, b, c, d in fours))
 
     def finish(j):
@@ -390,16 +358,16 @@
                 squares += jnp.sum((wide * wide).reshape(-1, 8, FT), 0)
         squares_ref[...] = squares
 
-    exchange_steps(exchange, loads, 2, compute, finish)
-
-
-def last_weights(at, byt, a2, by2, at2, byt2, act, dg, du, wg, wu, wd, layer):
+    exchange_steps(exchange, loads, 2, prepare, compute, finish)
+
+
+def last_weights(at, byt, h2, by2, act, dg, du, wg, wu, wd, layer):
     tile = pl.BlockSpec((T, FT), lambda j: (0, tile_now(j)))
     weight = pl.BlockSpec((None, D, FT), lambda j: (layer, 0, tile_now(j)))
     return pl.pallas_call(
         last_weights_kernel,
         grid=(NT + 2,),
-        in_specs=[ANY] * 6
+        in_specs=[ANY] * 4
         + [tile, tile, tile, weight, weight, pl.BlockSpec((None, FT, D), lambda j: (layer, tile_now(j), 0))],
         out_specs=[pl.BlockSpec((3, HALF, FT), lambda j: (0, 0, tile_done(j))), pl.BlockSpec((8, FT), lambda j: (0, 0))],
         out_shape=[jax.ShapeDtypeStruct((3, HALF, FF), BF), jax.ShapeDtypeStruct((8, FT), F32)],
@@ -407,13 +375,55 @@
             pltpu.VMEM((D, T), BF), pltpu.VMEM((D, T), BF), pltpu.VMEM((T, D), BF),
             pltpu.VMEM((T, D), BF), pltpu.VMEM((D, T), BF), pltpu.VMEM((D, T), BF),
             *[pltpu.VMEM((T, FT), BF)] * 3,
-            pltpu.SemaphoreType.DMA((6,)),
+            pltpu.SemaphoreType.DMA((4,)),
             *Exchange.scratch,
         ],
         compiler_params=params(collective_id=1),
         cost_estimate=cost(9, 90e6),
         name="last_weights",
-    )(at, byt, a2, by2, at2, byt2, act, dg, du, wg, wu, wd)
+    )(at, byt, h2, by2, act, dg, du, wg, wu, wd)
+
+
+def home_kernel(home_ref, far_ref, squares1_ref, left_ref, right_ref, squares_ref, total_ref):
+    j = pl.program_id(0)
+
+    @pl.when(j == 0)
+    def _():
+        total_ref[...] = jnp.zeros_like(total_ref)
+
+    for half, out_ref in enumerate((left_ref, right_ref)):
+        columns = slice(half * BROAD, (half + 1) * BROAD)
+
+        def some(r, total, columns=columns, out_ref=out_ref):
+            rows = part(r, 16)
+            mine = (home_ref[rows, columns] + far_ref[rows, columns].astype(F32)).astype(BF)
+            out_ref[rows, :] = mine
+            wide = mine.astype(F32)
+            wide = wide * wide
+            return total + wide[:8] + wide[8:]
+
+        total_ref[...] = lax.fori_loop(0, QUARTER // 32, some, total_ref[...], unroll=2)
+
+    @pl.when(j == pl.num_programs(0) - 1)
+    def _():
+        squares_ref[0, 0] = jnp.sum(total_ref[...])
+        squares_ref[0, 1] = jnp.sum(squares1_ref[...])
+
+
+def home_sum(home, far, squares1):
+    block = pl.BlockSpec((None, QUARTER // 2, FF), lambda s: (s // 2, s % 2, 0))
+    out = pl.BlockSpec((None, QUARTER // 2, BROAD), lambda s: (s // 2, s % 2, 0))
+    return pl.pallas_call(
+        home_kernel,
+        grid=(6,),
+        in_specs=[block, block, whole((8, FT))],
+        out_specs=[out, out, pl.BlockSpec(memory_space=pltpu.SMEM)],
+        out_shape=[jax.ShapeDtypeStruct((3, QUARTER, BROAD), BF)] * 2 + [jax.ShapeDtypeStruct((1, 2), F32)],
+        scratch_shapes=[pltpu.VMEM((8, BROAD), F32)],
+        compiler_params=params(),
+        cost_estimate=cost(0.2, 18e6),
+        name="home_sum",
+    )(home, far, squares1)
 
 
 def adamw(w, m, v, g):
@@ -508,33 +518,33 @@
 
         h0, by2 = x[0], dy[0]
         by2_other = swap_x(by2)
-        act0, gate0, up0, a0t = gate_up(h0, wg, wu, 0)
-        h1, a1, a1t = down(act0, wd, h0, 0)
+        act0, silu0, slope0, a0t, h1, a1, a1t = forward(h0, wg, wu, wd, 0)
         h1_other = swap_x(h1)
         act1, dg1, du1, by2t = hidden(a1, by2, wg, wu, wd, 1)
         by1, by1t = states(dg1, du1, wg, wu, h1, by2, 1)
-        home, away = first_weights(a0t, by1t, by1, gate0, up0, wd, 0)
+        home, away = first_weights(a0t, by1t, by1, act0, silu0, slope0, wd, 0)
         far = swap_x(away)
-        a1o, a1ot, by2ot = norm_turn(h1_other, by2_other)
-        half, squares1 = last_weights(a1t, by2t, a1o, by2_other, a1ot, by2ot, act1, dg1, du1, wg, wu, wd, 1)
+        half, squares1 = last_weights(a1t, by2t, h1_other, by2_other, act1, dg1, du1, wg, wu, wd, 1)
         core_half = swap_core(half)
-        quarter = (home + far.astype(F32)).astype(BF)
-        squares0 = jnp.sum(jnp.square(quarter.astype(F32)))
-
-        squares0 = squares0.reshape(1, 1)
-        squares0 = squares0 + swap_x(squares0)
-        squares = squares0 + jnp.sum(squares1).reshape(1, 1)
+        *quarter, squares = home_sum(home, far, squares1)
+
+        squares0, squares1 = squares[:, :1], squares[:, 1:]
+        squares = squares0 + swap_x(squares0) + squares1
         squares = (squares + swap_core(squares)).reshape(1)
         count = sum(a.size for a in arrays[:3])
         factor = jnp.minimum(1.0, 0.5 * lax.rsqrt(squares / count + 1e-30))
 
-        far_quarter = swap_x(quarter)
-        core_quarter = swap_core(quarter)
-        core_far = swap_core(far_quarter)
+        far_quarter = [swap_x(q) for q in quarter]
+        core_quarter = [swap_core(q) for q in quarter]
+        core_far = [swap_core(q) for q in far_quarter]
+
+        def columns(pieces, row):
+            return [(g, 0, row, n) for n, g in enumerate(pieces)]
 
         groups = [
-            [(half, 1, 0, 0), (quarter, 0, 0, 0), (core_half, 1, 2, 0), (core_quarter, 0, 2, 0)],
-            [(far_quarter, 0, 1, 0), (core_far, 0, 3, 0)],
+            [(half, 1, 0, 0), *columns(quarter, 0)],
+            [(core_half, 1, 2, 0), *columns(core_quarter, 2)],
+            [*columns(far_quarter, 1), *columns(core_far, 3)],
         ]
         steps = [adamw_steps(group) for group in groups]
         table = np.array(sum(steps, []), np.int32).T

time: 601 us -> 773 us (1.29)
  waiting for transfers between devices: 99.5 us -> 284 us
  other arithmetic: 10.8 us -> 0.67 us
    ppermute x5 -> x6, waiting for transfers between devices: 99.1 us -> 284 us  [swap_x(): return lax.ppermute(a, 'dp', X_SWAP)]
    reduce_sum x2 -> x0, other arithmetic: 10.2 us -> none  [the longest x1 9.55 us: step(): squares0 = jnp.sum(jnp.square(quarter.astype(F32)))]
    pallas_call x2 -> x3, Pallas kernels: 130 us -> 134 us  [adamw_blocks(): pl.pallas_call(functools.partial(adamw_kernel, ranges, len(so_far)), grid...]
    pallas_call x4 -> x3, Pallas kernels: 191 us -> 192 us  [the longest x1 128 us: last_weights(): pl.pallas_call(last_weights_kernel, grid=(NT + 2,), in_specs=[ANY] * 4 +...]
  transfers between devices with their start and end apart: 9 -> 12, of which waited for: 3 -> 5; matrix products, arithmetic and copies ran while one was open for 2% -> 0% of each run, Pallas kernels for 74% -> 33%
where the time goes in v3:
time: 773 us; the launch traced here: 772 us
  Pallas kernels  470 us (61%)
  waiting for transfers between devices  284 us (37%)
  starting transfers between devices  10.8 us (1%)
    ppermute x6, waiting for transfers between devices, swap_x(): return lax.ppermute(a, 'dp', X_SWAP)  284 us
    pallas_call x3, Pallas kernels, adamw_blocks(): pl.pallas_call(functools.partial(adamw_kernel, ranges, len(so_far)), grid...  134 us
    pallas_call x1, Pallas kernels, last_weights(): pl.pallas_call(last_weights_kernel, grid=(NT + 2,), in_specs=[ANY] * 4 +...  128 us
    pallas_call x1, Pallas kernels, first_weights(): pl.pallas_call(first_weights_kernel, grid=(NT + 2,), in_specs=[ANY, ANY,...  63.4 us
    pallas_call x1, Pallas kernels, forward(): pl.pallas_call(forward_kernel, grid=(NT + NC,), in_specs=[whole((T, D)),...  55.8 us
    pallas_call x1, Pallas kernels, hidden(): pl.pallas_call(hidden_kernel, grid=(NT,), in_specs=[whole((T, D)), whole(...  46.3 us
    pallas_call x1, Pallas kernels, states(): pl.pallas_call(states_kernel, grid=(T // tm,), in_specs=[hidden_rows, hid...  34.9 us
  transfers between devices with their start and end apart: 12, of which 5 were waited for; matrix products, arithmetic and copies ran while one was open for 0% of the time, Pallas kernels for 33%

profile of v3, /device:TPU:0, one launch (start us, length us, event | category | flops | bytes accessed | tf_op | source)
XLA Modules:
  0.0 772.5 jit_solution(16947660814200839593)
XLA Ops:
  0.6 55.8 %forward.1 = (bf16[11,2048,256]{2,1,0:T(8,128)(2,1)}, f32[11,2048,256]{2,1,0:T(8,128)}, f32[11,2048,256]{2,1,0:T(8,128)}, bf16[1024,2048]{1,0:T(8,128)(2,1)}, bf...) custom-call(bf16[2048,1024]{1,0:T(8,128)(2,1)} %bitcast.3, ...), custom_call_target="tpu_custom_call" | custom-call | flops 35433480192 | bytes 90000000 | tf_op jit(solution)/shard_map/forward/pallas_call | solution.py:105
  56.4 3.3 collective-permute-start.1
  59.7 0.0 collective-permute-start.2
  59.7 46.3 %hidden.1 = (bf16[2048,2816]{1,0:T(8,128)(2,1)}, bf16[2048,2816]{1,0:T(8,128)(2,1)}, bf16[2048,2816]{1,0:T(8,128)(2,1)}, bf16[1024,2048]{1,0:T(8,128)(2,1)}) custom-call(bf16[2048,1024]{1,0:T(8,128)(2,1)} %get-tuple-element.48.a_ref, bf16[2048,1024]{1,0:T(8,128)(2,1)} %bitcast.5, bf16[2,1024,2816]{2,1,0:T(8,128)(2,1)} %refs_4_.5, ...), custom_call_target="tpu_custom_call" | custom-call | flops 35433480192 | bytes 60000000 | tf_op jit(solution)/shard_map/hidden/pallas_call | solution.py:148
  106.0 34.9 %states.1 = (bf16[2048,1024]{1,0:T(8,128)(2,1)}, bf16[1024,2048]{1,0:T(8,128)(2,1)}) custom-call(bf16[2048,2816]{1,0:T(8,128)(2,1)} %get-tuple-element.49.dg_ref, bf16[2048,2816]{1,0:T(8,128)(2,1)} %get-tuple-element.50.du_ref, bf16[2,1024,2816]{2,1,0:T(8,128)(2,1)} %refs_4_.5, bf16[2,1024,2816]{2,1,0:T(8,128)(2,1)} %refs_5_.5, ...), custom_call_target="tpu_custom_call" | custom-call | flops 23622320128 | bytes 45000000 | tf_op jit(solution)/shard_map/states/pallas_call | solution.py:177
  140.9 10.5 %collective-permute-done.1.h2_any = bf16[2048,1024]{1,0:T(8,128)(2,1)} collective-permute-done((bf16[2048,1024]{1,0:T(8,128)(2,1)}, bf16[2048,1024]{1,0:T(8,128)(2,1)}, u32[]{:S(2)}, u32[]{:S(2)}) %collective-permute-start.1) | collective-permute-done | bytes 4194336 | tf_op jit(solution)/shard_map/ppermute | solution.py:514
  151.5 89.0 %collective-permute-done.2.by2_any = bf16[2048,1024]{1,0:T(8,128)(2,1)} collective-permute-done((bf16[2048,1024]{1,0:T(8,128)(2,1)}, bf16[2048,1024]{1,0:T(8,128)(2,1)}, u32[]{:S(2)}, u32[]{:S(2)}) %collective-permute-start.2) | collective-permute-done | bytes 4194336 | tf_op jit(solution)/shard_map/ppermute | solution.py:514
  240.5 127.8 %last_weights.1 = (bf16[3,512,2816]{2,1,0:T(8,128)(2,1)}, f32[8,256]{1,0:T(8,128)}) custom-call(bf16[1024,2048]{1,0:T(8,128)(2,1)} %get-tuple-element.59.at_any, bf16[1024,2048]{1,0:T(8,128)(2,1)} %get-tuple-element.60.byt_any, bf16[2048,1024]{1,0:T(8,128)(2,1)} %collective-permute-done.1.h2_any, bf16[2048,1024]{1,0:T(8,128)(2,1)} %collective-permute-done.2.by2_any, ...), custom_call_target="tpu_custom_call" | custom-call | flops 106300440576 | bytes 90000000 | tf_op jit(solution)/shard_map/last_weights/pallas_call | solution.py:367
  368.3 0.4 collective-permute-start.9
  368.7 63.4 %first_weights.1 = (f32[3,256,2816]{2,1,0:T(8,128)}, bf16[3,256,2816]{2,1,0:T(8,128)(2,1)}) custom-call(bf16[1024,2048]{1,0:T(8,128)(2,1)} %get-tuple-element.47.at_any, bf16[1024,2048]{1,0:T(8,128)(2,1)} %get-tuple-element.52.byt_any, bf16[2048,1024]{1,0:T(8,128)(2,1)} %get-tuple-element.53.by_any, bf16[11,2048,256]{2,1,0:T(8,128)(2,1)} %get-tuple-element.54.act_ref, ...), custom_call_target="tpu_custom_call" | custom-call | flops 47244640256 | bytes 80000000 | tf_op jit(solution)/shard_map/first_weights/pallas_call | solution.py:299
  432.1 0.0 copy-start.3
  432.1 0.0 copy-start.1
  432.1 0.0 copy-start.2
  432.2 1.8 collective-permute-start
  433.9 94.2 %collective-permute-done.far_ref = bf16[3,256,2816]{2,1,0:T(8,128)(2,1)} collective-permute-done((bf16[3,256,2816]{2,1,0:T(8,128)(2,1)}, bf16[3,256,2816]{2,1,0:T(8,128)(2,1)}, u32[]{:S(2)}, u32[]{:S(2)}) %collective-permute-start) | collective-permute-done | bytes 4325408 | tf_op jit(solution)/shard_map/ppermute | solution.py:514
  528.2 8.6 %home_sum.1 = (bf16[3,256,1408]{2,1,0:T(8,128)(2,1)}, bf16[3,256,1408]{2,1,0:T(8,128)(2,1)}, f32[1,2]{1,0:T(1,128)}) custom-call(f32[3,256,2816]{2,1,0:T(8,128)} %get-tuple-element.57.home_ref, bf16[3,256,2816]{2,1,0:T(8,128)(2,1)} %collective-permute-done.far_ref, f32[8,256]{1,0:T(8,128)} %get-tuple-element.62.squares1_ref), custom_call_target="tpu_custom_call" | custom-call | flops 2362232064 | bytes 18000000 | tf_op jit(solution)/shard_map/home_sum/pallas_call | solution.py:416
  536.8 1.7 collective-permute-start.5
  538.5 0.3 collective-permute-start.6
  538.8 0.0 collective-permute-start.10
  538.8 1.3 fusion
  540.1 1.7 collective-permute-start.3
  541.9 90.1 %collective-permute-done.3 = f32[1,1]{1,0:T(1,128)} collective-permute-done((f32[1,1]{1,0:T(1,128)}, f32[1,1]{1,0:T(1,128)}, u32[]{:S(2)}, u32[]{:S(2)}) %collective-permute-start.3) | collective-permute-done | bytes 36 | tf_op jit(solution)/shard_map/ppermute | solution.py:514
  633.9 0.8 collective-permute-start.4
  634.8 0.3 collective-permute-done.4
  635.1 0.2 collective-permute-start.11
  635.3 0.0 copy-done.3
  635.3 0.0 collective-permute-done.5.refs_0_
  635.3 0.3 collective-permute-start.7
  635.7 0.0 collective-permute-done.6.refs_1_
  635.7 0.2 collective-permute-start.8
  635.8 0.0 copy-done.1
  635.9 0.0 copy-done.2
  635.9 0.7 multiply_xor_fusion.table_ref
  637.3 49.7 %adamw.3 = (bf16[2,1024,2816]{2,1,0:T(8,128)(2,1)}, bf16[2,1024,2816]{2,1,0:T(8,128)(2,1)}, bf16[2,2816,1024]{2,1,0:T(8,128)(2,1)}, f32[2,1024,2816]{2,1,0:T(8,1...) custom-call(s32[3,16]{1,0:T(4,128)} %multiply_xor_fusion.table_ref, ...), custom_call_target="tpu_custom_call" | custom-call | flops 11072962560 | bytes 71250000 | tf_op jit(solution)/shard_map/adamw/pallas_call | solution.py:490
  686.9 0.0 collective-permute-done.10.refs_1_
  686.9 0.0 copy-start
  687.0 0.0 collective-permute-done.11.refs_2_
  687.0 0.0 collective-permute-done.9.refs_0_
  687.0 1.4 copy-done
  688.4 49.6 %adamw.4 = (bf16[2,1024,2816]{2,1,0:T(8,128)(2,1)}, bf16[2,1024,2816]{2,1,0:T(8,128)(2,1)}, bf16[2,2816,1024]{2,1,0:T(8,128)(2,1)}, f32[2,1024,2816]{2,1,0:T(8,1...) custom-call(s32[3,16]{1,0:T(4,128)} %multiply_xor_fusion.table_ref, ...), custom_call_target="tpu_custom_call", output_to_operand_aliasing={{0}: (14, {}), {1}: (15, {}), {2}: (16, {}), {3}: (17, {}),... | custom-call | flops 11072962560 | bytes 71250000 | tf_op jit(solution)/shard_map/adamw/pallas_call | solution.py:490
  738.0 0.0 collective-permute-done.7.refs_2_
  738.0 0.0 collective-permute-done.8.refs_3_
  738.0 34.3 %adamw.5 = (bf16[2,1024,2816]{2,1,0:T(8,128)(2,1)}, bf16[2,1024,2816]{2,1,0:T(8,128)(2,1)}, bf16[2,2816,1024]{2,1,0:T(8,128)(2,1)}, f32[2,1024,2816]{2,1,0:T(8,1...) custom-call(s32[3,16]{1,0:T(4,128)} %multiply_xor_fusion.table_ref, ...), custom_call_target="tpu_custom_call", output_to_operand_aliasing={{0}: (15, {}), {1}: (16, {}), {2}: (17, {}), {3}: (18, {}),... | custom-call | flops 7381975040 | bytes 47500000 | tf_op jit(solution)/shard_map/adamw/pallas_call | solution.py:490
  (1 shorter events, 0.0 us)
Async XLA Ops:
  56.4 95.0 %collective-permute-start.1 = (bf16[2048,1024]{1,0:T(8,128)(2,1)}, bf16[2048,1024]{1,0:T(8,128)(2,1)}, u32[]{:S(2)}, u32[]{:S(2)}) collective-permute-start(bf16[2048,1024]{1,0:T(8,128)(2,1)} %get-tuple-element.51.h_ref), channel_id=1, source_target_pairs={{0,2},{2,0},{1,3},{3,1},{4,6},{6,4},{5,7},{7,5}} | collective-permute-start | bytes 12582920 | tf_op jit(solution)/shard_map/ppermute | solution.py:514
  59.7 180.8 %collective-permute-start.2 = (bf16[2048,1024]{1,0:T(8,128)(2,1)}, bf16[2048,1024]{1,0:T(8,128)(2,1)}, u32[]{:S(2)}, u32[]{:S(2)}) collective-permute-start(bf16[2048,1024]{1,0:T(8,128)(2,1)} %bitcast.4), channel_id=1, source_target_pairs={{0,2},{2,0},{1,3},{3,1},{4,6},{6,4},{5,7},{7,5}} | collective-permute-start | bytes 12582920 | tf_op jit(solution)/shard_map/ppermute | solution.py:514
  368.3 318.6 %collective-permute-start.9 = (bf16[3,512,2816]{2,1,0:T(8,128)(2,1)}, bf16[3,512,2816]{2,1,0:T(8,128)(2,1)}, u32[]{:S(2)}, u32[]{:S(2)}) collective-permute-start(bf16[3,512,2816]{2,1,0:T(8,128)(2,1)} %get-tuple-element.66.refs_0_), channel_id=1, source_target_pairs={{0,1},{1,0},{2,3},{3,2},{4,5},{5,4},{6,7},{7,6}} | collective-permute-start | bytes 25952264 | tf_op jit(solution)/shard_map/ppermute | solution.py:517
  432.1 203.2 %copy-start.3 = (pred[16]{0:T(512)(128)(4,1)S(1)}, pred[16]{0:T(512)(128)(4,1)}, u32[]{:S(2)}) copy-start(pred[16]{0:T(512)(128)(4,1)} %constant.26.clone) | copy-start | bytes 52
  432.1 203.7 %copy-start.1 = (s32[3,16]{1,0:T(4,128)S(1)}, s32[3,16]{1,0:T(4,128)}, u32[]{:S(2)}) copy-start(s32[3,16]{1,0:T(4,128)} %constant.27.clone) | copy-start | bytes 580
  432.1 203.7 %copy-start.2 = (s32[3]{0:T(128)S(1)}, s32[3]{0:T(128)}, u32[]{:S(2)}) copy-start(s32[3]{0:T(128)} %constant.31) | copy-start | bytes 40
  432.2 96.0 %collective-permute-start = (bf16[3,256,2816]{2,1,0:T(8,128)(2,1)}, bf16[3,256,2816]{2,1,0:T(8,128)(2,1)}, u32[]{:S(2)}, u32[]{:S(2)}) collective-permute-start(bf16[3,256,2816]{2,1,0:T(8,128)(2,1)} %get-tuple-element.58), channel_id=1, source_target_pairs={{0,2},{2,0},{1,3},{3,1},{4,6},{6,4},{5,7},{7,5}} | collective-permute-start | bytes 12976136 | tf_op jit(solution)/shard_map/ppermute | solution.py:514
  536.8 98.5 %collective-permute-start.5 = (bf16[3,256,1408]{2,1,0:T(8,128)(2,1)}, bf16[3,256,1408]{2,1,0:T(8,128)(2,1)}, u32[]{:S(2)}, u32[]{:S(2)}) collective-permute-start(bf16[3,256,1408]{2,1,0:T(8,128)(2,1)} %get-tuple-element.64.refs_1_), channel_id=1, source_target_pairs={{0,2},{2,0},{1,3},{3,1},{4,6},{6,4},{5,7},{7,5}} | collective-permute-start | bytes 6488072 | tf_op jit(solution)/shard_map/ppermute | solution.py:514
  538.5 97.1 %collective-permute-start.6 = (bf16[3,256,1408]{2,1,0:T(8,128)(2,1)}, bf16[3,256,1408]{2,1,0:T(8,128)(2,1)}, u32[]{:S(2)}, u32[]{:S(2)}) collective-permute-start(bf16[3,256,1408]{2,1,0:T(8,128)(2,1)} %get-tuple-element.65.refs_2_), channel_id=1, source_target_pairs={{0,2},{2,0},{1,3},{3,1},{4,6},{6,4},{5,7},{7,5}} | collective-permute-start | bytes 6488072 | tf_op jit(solution)/shard_map/ppermute | solution.py:514
  538.8 148.1 %collective-permute-start.10 = (bf16[3,256,1408]{2,1,0:T(8,128)(2,1)}, bf16[3,256,1408]{2,1,0:T(8,128)(2,1)S(1)}, u32[]{:S(2)}, u32[]{:S(2)}) collective-permute-start(bf16[3,256,1408]{2,1,0:T(8,128)(2,1)} %get-tuple-element.64.refs_1_), channel_id=1, source_target_pairs={{0,1},{1,0},{2,3},{3,2},{4,5},{5,4},{6,7},{7,6}} | collective-permute-start | bytes 6488072 | tf_op jit(solution)/shard_map/ppermute | solution.py:517
  540.1 91.9 %collective-permute-start.3 = (f32[1,1]{1,0:T(1,128)}, f32[1,1]{1,0:T(1,128)}, u32[]{:S(2)}, u32[]{:S(2)}) collective-permute-start(f32[1,1]{1,0:T(1,128)} %get-tuple-element.86), channel_id=1, source_target_pairs={{0,2},{2,0},{1,3},{3,1},{4,6},{6,4},{5,7},{7,5}} | collective-permute-start | bytes 20 | tf_op jit(solution)/shard_map/ppermute | solution.py:514
  633.9 1.2 collective-permute-start.4
  635.1 51.8 %collective-permute-start.11 = (bf16[3,256,1408]{2,1,0:T(8,128)(2,1)}, bf16[3,256,1408]{2,1,0:T(8,128)(2,1)}, u32[]{:S(2)}, u32[]{:S(2)}) collective-permute-start(bf16[3,256,1408]{2,1,0:T(8,128)(2,1)} %get-tuple-element.65.refs_2_), channel_id=1, source_target_pairs={{0,1},{1,0},{2,3},{3,2},{4,5},{5,4},{6,7},{7,6}} | collective-permute-start | bytes 6488072 | tf_op jit(solution)/shard_map/ppermute | solution.py:517
  635.3 102.7 %collective-permute-start.7 = (bf16[3,256,1408]{2,1,0:T(8,128)(2,1)}, bf16[3,256,1408]{2,1,0:T(8,128)(2,1)}, u32[]{:S(2)}, u32[]{:S(2)}) collective-permute-start(bf16[3,256,1408]{2,1,0:T(8,128)(2,1)} %collective-permute-done.5.refs_0_), channel_id=1, source_target_pairs={{0,1},{1,0},{2,3},{3,2},{4,5},{5,4},{6,7},{7,6}} | collective-permute-start | bytes 6488072 | tf_op jit(solution)/shard_map/ppermute | solution.py:517
  635.7 102.4 %collective-permute-start.8 = (bf16[3,256,1408]{2,1,0:T(8,128)(2,1)}, bf16[3,256,1408]{2,1,0:T(8,128)(2,1)}, u32[]{:S(2)}, u32[]{:S(2)}) collective-permute-start(bf16[3,256,1408]{2,1,0:T(8,128)(2,1)} %collective-permute-done.6.refs_1_), channel_id=1, source_target_pairs={{0,1},{1,0},{2,3},{3,2},{4,5},{5,4},{6,7},{7,6}} | collective-permute-start | bytes 6488072 | tf_op jit(solution)/shard_map/ppermute | solution.py:517
  686.9 1.5 copy-start
